TPU v7x, 32 devices: a whole 2x2x4 slice. The times are simulated.
32 devices in a mesh: groups: 2 (over x), seq: 16 (over z, y, core).
Axes of the slice: x: 2, y: 2, z: 4, core: 2. Of those that a mesh axis runs over, the one named last changes fastest.
Arguments:
- attn_query: bfloat16 [8192, 2048], P(('groups', 'seq')), parts along dimension 0, may hold values from -16 to 16
- attn_key: bfloat16 [8192, 2048], P(('groups', 'seq')), parts along dimension 0, may hold values from -16 to 16
- attn_value: bfloat16 [8192, 2048], P(('groups', 'seq')), parts along dimension 0, may hold values from -6 to 6
- mesa_query: bfloat16 [8192, 2048], P(('groups', 'seq')), parts along dimension 0, may hold values from -6 to 6
- mesa_key: bfloat16 [8192, 2048], P(('groups', 'seq')), parts along dimension 0, may hold values from -16 to 16
- log_decay: float32 [8192, 16], P(('groups', 'seq')), parts along dimension 0, may hold values from -1 to 0
- input_gate: float32 [8192, 16], P(('groups', 'seq')), parts along dimension 0, may hold values from 0.2 to 1
- regularizer: float32 [16, 128], replicated, may hold values from 0.5 to 4
Outputs:
- attention: bfloat16 [8192, 2048], P(('groups', 'seq')), parts along dimension 0
- mesa_out: bfloat16 [8192, 2048], P(('groups', 'seq')), parts along dimension 0
There are 2 independent parts, one for each index of `groups`. A program takes and returns all parts, laid end to end along the dimension named above; an argument that names none is the same for every part. Nothing has to cross between parts.
All inputs are finite; a program needn't handle non-finite values.
Results may differ from a plain program's by a relative error of at most 0.017.
Values may be sent and summed in bfloat16 or wider, within the bound.
A program may use at most 128 MiB of HBM per device.

v0:
```python
import jax
import jax.numpy as jnp
from jax import lax
from jax.experimental import pallas as pl
from jax.experimental.pallas import tpu as pltpu
from jax.sharding import PartitionSpec as P
import functools
import math

WINDOW = 2048
SPAN = 64
CG_ITERS = 8


exact_mode = lax.Precision.HIGHEST
masked_score = -1e30


def prefix(shard, axis, join, neutral):
    place = lax.axis_index(axis)
    gathered = jax.tree.map(
        lambda a, kind: lax.all_gather(a.astype(kind), axis), shard, (jnp.bfloat16, jnp.bfloat16)
    )
    state = jax.tree.map(lambda a, e: jnp.zeros_like(a) + jnp.asarray(e, a.dtype), shard, neutral)

    def one(lap, state):
        return join(
            state,
            jax.tree.map(
                lambda a, own: lax.dynamic_index_in_dim(a, lap, 0, False).astype(own.dtype),
                gathered,
                shard,
            ),
        )

    return lax.fori_loop(0, place, one, state)


def passed_along(value, axis, steps):
    count = lax.axis_size(axis)
    first, last = (max(0, -steps), min(count, count - steps))
    return lax.ppermute(value, axis, [(source, source + steps) for source in range(first, last)])


def span_update(states, inputs, ridge_diag):
    gram_start, cross_start = states
    queries, key_rows, value_rows, log_rates, gate_rows = inputs
    q_heads = jnp.transpose(queries, (1, 0, 2))
    k_heads = jnp.transpose(key_rows, (1, 0, 2))
    v_heads = jnp.transpose(value_rows, (1, 0, 2))
    cumulative = jnp.transpose(jnp.cumsum(log_rates, axis=0))
    length = cumulative.shape[1]
    causal = (jnp.arange(length)[:, None] >= jnp.arange(length)[None, :])[None]
    distance = cumulative[:, :, None] - cumulative[:, None, :]
    decay_mix = (
        jnp.where(causal, jnp.exp(jnp.where(causal, distance, 0.0)), 0.0)
        * jnp.transpose(gate_rows)[:, None, :]
    )
    start_scale = jnp.exp(cumulative)[:, :, None]
    iterate = jnp.zeros_like(q_heads)
    remain = q_heads
    search = q_heads
    norm_now = jnp.sum(remain * remain, axis=-1, keepdims=True)
    for sweep_index in range(CG_ITERS):
        carried = start_scale * jnp.einsum("hcd,hed->hce", search, gram_start, precision=exact_mode)
        operator_products = jnp.einsum("hjd,hid->hji", search, k_heads, precision=exact_mode)
        local_part = jnp.einsum(
            "hji,hid->hjd", decay_mix * operator_products, k_heads, precision=exact_mode
        )
        image_vec = carried + local_part + ridge_diag[:, None, :] * search
        step_size = norm_now / (jnp.sum(search * image_vec, axis=-1, keepdims=True) + 1e-06)
        iterate = iterate + step_size * search
        remain = remain - step_size * image_vec
        norm_next = jnp.sum(remain * remain, axis=-1, keepdims=True)
        search = remain + norm_next / (norm_now + 1e-06) * search
        norm_now = norm_next
    products = jnp.einsum("hjd,hid->hji", iterate, k_heads, precision=exact_mode)
    mesa_rows = start_scale * jnp.einsum("hje,hde->hjd", iterate, cross_start, precision=exact_mode)
    mesa_rows = mesa_rows + jnp.einsum(
        "hji,hid->hjd", decay_mix * products, v_heads, precision=exact_mode
    )
    tail_weight = (jnp.exp(cumulative[:, -1:] - cumulative) * jnp.transpose(gate_rows))[:, :, None]
    end_scale = jnp.exp(cumulative[:, -1])[:, None, None]
    gram_end = end_scale * gram_start + jnp.einsum(
        "hid,hie->hde", k_heads * tail_weight, k_heads, precision=exact_mode
    )
    cross_end = end_scale * cross_start + jnp.einsum(
        "hid,hie->hde", v_heads * tail_weight, k_heads, precision=exact_mode
    )
    return ((gram_end, cross_end), jnp.transpose(mesa_rows, (1, 0, 2)))


def mesa_pass(
    queries, key_rows, value_rows, log_rates, gate_rows, ridge_diag, gram_start, cross_start
):
    row_total = queries.shape[0]
    span_count = row_total // SPAN

    def shaped(array_in):
        return array_in.reshape((span_count, SPAN) + array_in.shape[1:])

    def advance(states, inputs):
        return span_update(states, inputs, ridge_diag)

    finished, outputs = lax.scan(
        advance,
        (gram_start, cross_start),
        (
            shaped(queries),
            shaped(key_rows),
            shaped(value_rows),
            shaped(log_rates),
            shaped(gate_rows),
        ),
    )
    return outputs.reshape(row_total, -1)


def fold_block(state_now, queries, key_value, query_first, key_first):
    running_max, running_sum, weighted = state_now
    row_count, head_count, head_size = queries.shape
    key_rows = key_value[0].reshape(-1, head_count, head_size)
    value_rows = key_value[1].reshape(-1, head_count, head_size)
    scores = jnp.einsum(
        "qhd,khd->hqk", queries, key_rows, preferred_element_type=jnp.float32
    ) * head_size ** (-0.5)
    query_pos = query_first + jnp.arange(row_count, dtype=jnp.int32)[:, None]
    key_pos = key_first + jnp.arange(key_rows.shape[0], dtype=jnp.int32)[None, :]
    distance = query_pos - key_pos
    inside = ((distance >= 0) & (distance < WINDOW) & (key_pos >= 0))[None]
    scores = jnp.where(inside, scores, masked_score)
    new_max = jnp.maximum(running_max, jnp.max(scores, axis=-1))
    weights = jnp.exp(scores - new_max[:, :, None]) * inside.astype(jnp.float32)
    rescale = jnp.exp(running_max - new_max)
    running_sum = running_sum * rescale + jnp.sum(weights, axis=-1)
    weighted = weighted * rescale[:, :, None] + jnp.einsum(
        "hqk,khd->hqd", weights.astype(jnp.bfloat16), value_rows, preferred_element_type=jnp.float32
    )
    return (new_max, running_sum, weighted)


def combine_pair(earlier, later):
    return (earlier[0] + later[0], jnp.exp(later[0])[:, None, None] * earlier[1] + later[1])


def slab_body(
    attn_query, attn_key, attn_value, mesa_query, mesa_key, log_decay, input_gate, regularizer
):
    row_count = attn_query.shape[0]
    head_count, head_size = regularizer.shape
    shape3 = (row_count, head_count, head_size)
    slab_first = lax.axis_index("seq") * row_count
    keys_float = mesa_key.astype(jnp.float32).reshape(shape3)
    slab_log = jnp.sum(log_decay, axis=0)
    tail_log = slab_log[None, :] - jnp.cumsum(log_decay, axis=0)
    weight_rows = (jnp.exp(tail_log) * input_gate)[:, :, None]
    gram_local = jnp.einsum(
        "lhd,lhe->hde", keys_float * weight_rows, keys_float, precision=exact_mode
    )
    zero_log = jnp.zeros_like(slab_log)
    zero_state = jnp.zeros_like(gram_local)
    gram_prefix = prefix((slab_log, gram_local), "seq", combine_pair, (zero_log, zero_state))[1]
    queries = attn_query.reshape(shape3)
    key_value = jnp.stack([attn_key, attn_value])
    state_now = (
        jnp.full((head_count, row_count), masked_score, jnp.float32),
        jnp.zeros((head_count, row_count), jnp.float32),
        jnp.zeros((head_count, row_count, head_size), jnp.float32),
    )
    state_now = fold_block(state_now, queries, key_value, slab_first, slab_first)
    reach = -(-WINDOW // row_count)
    moving = key_value
    for hop_index in range(1, reach + 1):
        moving = passed_along(moving, "seq", 1)
        state_now = fold_block(
            state_now, queries, moving, slab_first, slab_first - hop_index * row_count
        )
    normed = state_now[2] / state_now[1][:, :, None]
    attention = jnp.transpose(normed, (1, 0, 2)).reshape(row_count, -1).astype(jnp.bfloat16)
    values_float = attention.astype(jnp.float32).reshape(shape3)
    cross_local = jnp.einsum(
        "lhd,lhe->hde", values_float * weight_rows, keys_float, precision=exact_mode
    )
    cross_prefix = prefix((slab_log, cross_local), "seq", combine_pair, (zero_log, zero_state))[1]
    mesa_out = mesa_pass(
        mesa_query.astype(jnp.float32).reshape(shape3),
        keys_float,
        values_float,
        log_decay,
        input_gate,
        regularizer,
        gram_prefix,
        cross_prefix,
    )
    return (attention, mesa_out.astype(jnp.bfloat16))


CHUNK = 128
WAYS = 4
BF16 = jnp.bfloat16
F32 = jnp.float32
NT = (((1,), (1,)), ((), ()))
TN = (((0,), (0,)), ((), ()))


def dot(a, b, dims=None):
    if dims is None:
        return jnp.dot(a, b, preferred_element_type=F32)
    return lax.dot_general(a, b, dims, preferred_element_type=F32)


def two_terms(a):
    high = a.astype(BF16)
    low = (a - high.astype(F32)).astype(BF16)
    return jnp.concatenate([high, low], axis=1)


def attend_block(q_ref, k_ref, v_ref, out_ref, i, first, count, rows, banded):
    scale = math.log2(math.e) / math.sqrt(q_ref.shape[1])
    queries = q_ref[pl.ds(pl.multiple_of(i * rows, rows), rows), :]
    base = pl.multiple_of(first * rows, rows)
    row = lax.broadcasted_iota(jnp.int32, (rows, rows), 0)
    col = lax.broadcasted_iota(jnp.int32, (rows, rows), 1)
    scores, top = [], None
    for j in range(count):
        s = dot(queries, k_ref[pl.ds(base + j * rows, rows), :], NT)
        if banded and j == 0:
            s = jnp.where(row - col + (count - 1) * rows < WINDOW, s, masked_score)
        if j == count - 1 or (not banded and j == count - 2):
            s = jnp.where(row - col + (i - first - j) * rows >= 0, s, masked_score)
        scores.append(s)
        top = s if top is None else jnp.maximum(top, s)
    top = jnp.max(top, axis=1, keepdims=True)
    total, weights = None, []
    for s in scores:
        w = jnp.exp2((s - top) * scale)
        total = w if total is None else total + w
        weights.append(w.astype(BF16))
    total = jnp.sum(total, axis=1, keepdims=True)
    summed = dot(
        jnp.concatenate(weights, axis=1), v_ref[pl.ds(base, count * rows), :]
    )
    out_ref[pl.ds(pl.multiple_of(i * rows, rows), rows), :] = (summed / total).astype(BF16)


def attend_all(q_ref, k_ref, v_ref, out_ref, rows, order, done):
    blocks = q_ref.shape[0] // rows
    reach = WINDOW // rows
    early = min(reach, blocks)

    def one(t, carry):
        i = order(t)
        for low in range(0, early, 2):
            high = min(low + 2, early)

            @pl.when((i >= low) & (i < high))
            def _(high=high):
                attend_block(q_ref, k_ref, v_ref, out_ref, i, 0, high, rows, False)

        if blocks > reach:

            @pl.when(i >= reach)
            def _():
                attend_block(q_ref, k_ref, v_ref, out_ref, i, i - reach, reach + 1, rows, True)

        done(i)
        return carry

    lax.fori_loop(0, blocks, one, 0)


def flat(c, per):
    return c[0] * per + c[1]


def span(c, per):
    return pl.ds(pl.multiple_of(flat(c, per) * CHUNK, CHUNK), CHUNK)


def chunk_ids(g, per, ways=WAYS):
    slabs = ways // per
    return [(g * slabs + w // per, w % per) for w in range(ways)]


def column_form(row):
    return jnp.transpose(jnp.broadcast_to(row, (CHUNK, CHUNK)))


def rates_of(rates_ref, c):
    slab, place = c
    per = rates_ref.shape[1] // 4
    return rates_ref[slab, place : place + 1, :], rates_ref[slab, per + place : per + place + 1, :]


def tail_keys(k_ref, rates_ref, c, per):
    cum, gate = rates_of(rates_ref, c)
    weight = column_form(jnp.exp(cum[:, CHUNK - 1 :] - cum) * gate)
    keys = k_ref[span(c, per), :]
    return (keys.astype(F32) * weight).astype(BF16), jnp.exp(cum[:, CHUNK - 1 :])


def mix_of(rates_ref, c):
    cum, gate = rates_of(rates_ref, c)
    col = column_form(cum)
    shape = (CHUNK, CHUNK)
    causal = lax.broadcasted_iota(jnp.int32, shape, 0) >= lax.broadcasted_iota(
        jnp.int32, shape, 1
    )
    mix = jnp.exp(jnp.where(causal, col - cum, masked_score)) * gate
    return mix, jnp.exp(col)


def gram_states(k_ref, other_ref, rates_ref, starts_ref):
    per = rates_ref.shape[1] // 4
    chunks = rates_ref.shape[0] * per

    def step(g, state):
        for c in chunk_ids(g, per):
            starts_ref[flat(c, per)] = state.astype(BF16)
            keys, end = tail_keys(k_ref, rates_ref, c, per)
            state = end * state + dot(keys, other_ref[span(c, per), :], TN)
        return state

    lax.fori_loop(0, chunks // WAYS, step, jnp.zeros((CHUNK, CHUNK), F32))


def solve_all(q_ref, k_ref, rates_ref, ridge_ref, gram_ref, x_ref):
    ridge = ridge_ref
    per = rates_ref.shape[1] // 4
    chunks = rates_ref.shape[0] * per

    def group(g, carry):
        ids = chunk_ids(g, per)
        mixes = [mix_of(rates_ref, c) for c in ids]
        keys = [k_ref[span(c, per), :] for c in ids]
        grams = [gram_ref[flat(c, per)] for c in ids]
        sides = [
            jnp.concatenate(
                [jnp.concatenate([a, a], axis=1), jnp.concatenate([k, k], axis=1)], axis=0
            )
            for a, k in zip(grams, keys)
        ]
        stacks = [jnp.concatenate([k, k], axis=0) for k in keys]
        state = []
        for c in ids:
            q = q_ref[span(c, per), :].astype(F32)
            state.append((jnp.zeros_like(q), q, q, jnp.sum(q * q, axis=1, keepdims=True)))

        def sweep(n, state):
            both = [dot(two_terms(s[2]), side, NT) for s, side in zip(state, sides)]
            local = [
                dot(two_terms(m[0] * b[:, CHUNK:]), k) for m, b, k in zip(mixes, both, stacks)
            ]
            out = []
            for (x, r, p, rr), b, l, m in zip(state, both, local, mixes):
                a = m[1] * b[:, :CHUNK] + l + ridge * p
                alpha = rr / (jnp.sum(p * a, axis=1, keepdims=True) + 1e-6)
                x = x + alpha * p
                r = r - alpha * a
                new = jnp.sum(r * r, axis=1, keepdims=True)
                p = r + (new / (rr + 1e-6)) * p
                out.append((x, r, p, new))
            return tuple(out)

        state = lax.fori_loop(0, CG_ITERS, sweep, tuple(state))
        for c, s in zip(ids, state):
            x_ref[span(c, per), :] = s[0]
        return carry

    lax.fori_loop(0, chunks // WAYS, group, 0)


def read_out(k_ref, v_ref, rates_ref, cross_ref, x_ref, out_ref, slab):
    per = rates_ref.shape[1] // 4
    for c in chunk_ids(slab, per, per):
        mix, start = mix_of(rates_ref, c)
        keys, values, cross = k_ref[span(c, per), :], v_ref[span(c, per), :], cross_ref[flat(c, per)]
        x = two_terms(x_ref[span(c, per), :])
        products = dot(x, jnp.concatenate([keys, keys], axis=1), NT)
        rows = start * dot(x, jnp.concatenate([cross, cross], axis=0))
        rows = rows + dot(two_terms(mix * products), jnp.concatenate([values, values], axis=0))
        out_ref[span(c, per), :] = rows.astype(BF16)


def head_kernel(n, *refs):
    ins, rates_in, ridge_in = refs[:5], refs[5], refs[6]
    results = refs[7:9]
    bufs, rates, homes = refs[9:14], refs[14], refs[15:17]
    gram, cross, x = refs[17:20]
    send, recv, own = refs[20:23]
    q, k, v, mk, mq = bufs
    att, out = homes
    rows, size = ins[0].shape[0], ridge_in.shape[1]
    group, me = lax.axis_index("groups"), lax.axis_index("seq")

    def row_block(ref, s):
        return ref.at[pl.ds(pl.multiple_of(s * rows, rows), rows), :]

    def col_block(ref, h):
        return ref.at[:, pl.ds(pl.multiple_of(h * size, size), size)]

    def ends(a, source, target):
        if a < 5:
            return col_block(ins[a], target), row_block(bufs[a], source)
        if a == 5:
            return rates_in.at[target], rates.at[source]
        return row_block(homes[a - 6], target), col_block(results[a - 6], source)

    def remote(a, source, target, peer):
        src, dst = ends(a, source, target)
        return pltpu.make_async_remote_copy(
            src_ref=src,
            dst_ref=dst,
            send_sem=send.at[a, target],
            recv_sem=recv.at[a, source],
            device_id=(group, peer),
            device_id_type=pl.DeviceIdType.MESH,
        )

    def local(a):
        src, dst = ends(a, me, me)
        return pltpu.make_async_copy(src, dst, own.at[a])

    def other(t):
        return lax.rem(me + t, n)

    def over_peers(act):
        def one(t, carry):
            act(other(t))
            return carry

        lax.fori_loop(1, n, one, 0)

    def arrive(a):
        over_peers(lambda peer: remote(a, peer, me, peer).wait_recv())
        local(a).wait()

    def give(a, slab):
        @pl.when(slab != me)
        def _():
            remote(a, me, slab, slab).start()

        @pl.when(slab == me)
        def _():
            local(a).start()

    barrier = pltpu.get_barrier_semaphore()
    over_peers(
        lambda peer: pl.semaphore_signal(
            barrier, inc=1, device_id=(group, peer), device_id_type=pl.DeviceIdType.MESH
        )
    )
    pl.semaphore_wait(barrier, n - 1)
    for a in SEND_ORDER:
        over_peers(lambda peer: remote(a, me, peer, peer).start())
        local(a).start()

    for a in (5, 3, 4):
        arrive(a)
    gram_states(mk, mk, rates, gram)
    solve_all(mq, mk, rates, ridge_in[pl.ds(me, 1), :], gram, x)
    for a in (0, 1, 2):
        arrive(a)
    attend_all(q, k, v, att, rows, lambda t: other(t + 1), lambda i: give(6, i))
    gram_states(mk, att, rates, cross)

    def slab_out(t, carry):
        slab = other(t + 1)
        read_out(mk, att, rates, cross, x, out, slab)
        give(7, slab)
        return carry

    lax.fori_loop(0, n, slab_out, 0)
    for a in (6, 7):
        arrive(a)
    for a in range(8):
        over_peers(lambda peer: remote(a, me, peer, peer).wait_send())


SEND_ORDER = (5, 3, 4, 0, 1, 2)


def head_body(
    attn_query, attn_key, attn_value, mesa_query, mesa_key, log_decay, input_gate, regularizer
):
    rows = attn_query.shape[0]
    heads, size = regularizer.shape
    devices = lax.axis_size("seq")
    tokens = rows * devices
    per, chunks = rows // CHUNK, tokens // CHUNK
    cum = jnp.cumsum(log_decay.reshape(per, CHUNK, heads), axis=1)
    rates = jnp.concatenate([cum, input_gate.reshape(per, CHUNK, heads)], axis=0)
    rates = jnp.pad(jnp.transpose(rates, (2, 0, 1)), ((0, 0), (0, 2 * per), (0, 0)))
    slab = jax.ShapeDtypeStruct((rows, heads * size), BF16)
    vmem = pl.BlockSpec(memory_space=pltpu.VMEM)
    anywhere = pl.BlockSpec(memory_space=pl.ANY)
    return pl.pallas_call(
        functools.partial(head_kernel, devices),
        out_shape=(slab, slab),
        in_specs=[anywhere] * 5 + [vmem] * 2,
        out_specs=(anywhere, anywhere),
        scratch_shapes=[pltpu.VMEM((tokens, size), BF16)] * 5
        + [pltpu.VMEM((devices, 4 * per, CHUNK), F32)]
        + [pltpu.VMEM((tokens, size), BF16)] * 2
        + [pltpu.VMEM((chunks, size, size), BF16)] * 2
        + [
            pltpu.VMEM((tokens, size), F32),
            pltpu.SemaphoreType.DMA((8, devices)),
            pltpu.SemaphoreType.DMA((8, devices)),
            pltpu.SemaphoreType.DMA((8,)),
        ],
        compiler_params=pltpu.CompilerParams(
            collective_id=0, has_side_effects=True, vmem_limit_bytes=56 * 1024 * 1024
        ),
    )(attn_query, attn_key, attn_value, mesa_key, mesa_query, rates, regularizer)


def fits_heads(mesh, rows, heads, size):
    tokens = rows * mesh.shape["seq"]
    return (
        mesh.shape["seq"] == heads
        and size == CHUNK
        and WINDOW % rows == 0
        and rows % CHUNK == 0
        and WAYS % (rows // CHUNK) == 0
        and tokens % (CHUNK * WAYS) == 0
    )


def solution(mesh):
    spec = P(("groups", "seq"), None)

    def body(*args):
        heads, size = args[7].shape
        chosen = head_body if fits_heads(mesh, args[0].shape[0], heads, size) else slab_body
        return chosen(*args)

    return jax.shard_map(
        body,
        mesh=mesh,
        in_specs=(spec,) * 7 + (P(),),
        out_specs=(spec, spec),
        check_vma=False,
    )
```

profile of v0, /device:TPU:29, one launch (start us, length us, event | category | flops | bytes accessed | tf_op | source)
XLA Modules:
  0.0 180.4 jit_solution(4610393513713693110)
XLA Ops:
  0.6 0.0 copy-start.1
  0.6 0.7 reshape.11
  1.4 0.0 copy-done.1
  1.4 0.1 copy.12
  1.5 0.2 reduce_window_sum.11
  1.7 0.1 copy.11
  1.8 0.6 pad.4.refs_5_
  2.4 174.6 %shard_map.95 = (bf16[256,2048]{1,0:T(8,128)(2,1)}, bf16[256,2048]{1,0:T(8,128)(2,1)}) custom-call(bf16[256,2048]{1,0:T(8,128)(2,1)} %refs_0_.1, bf16[256,2048]{1,0:T(8,128)(2,1)} %refs_1_.1, bf16[256,2048]{1,0:T(8,128)(2,1)} %refs_2_.1, bf16[256,2048]{1,0:T(8,128)(2,1)} %refs_3_.1, bf16[256,2048]{1,0:T(8,128)(2,1)} %refs_4_.1, f32[16,8,128]{2,1,0:T(8,128)} %pad.4.refs_5_, ...), custom_call_target="tpu_custom_call" | custom-call | tf_op jit(solution)/shard_map/pallas_call | solution.py:497
  177.0 0.0 copy-start
  177.0 2.4 %copy.15 = bf16[256,2048]{1,0:T(8,128)(2,1)} copy(bf16[256,2048]{1,0:T(8,128)(2,1)} %get-tuple-element.4) | data formatting | bytes 2097152
  179.4 0.0 copy-done
  179.4 1.0 copy.16
  (1 shorter events, 0.0 us)
Async XLA Ops:
  0.6 0.7 copy-start.1
  177.0 2.4 %copy-start = (bf16[256,2048]{1,0:T(8,128)(2,1)S(1)}, bf16[256,2048]{1,0:T(8,128)(2,1)}, u32[]{:S(2)}) copy-start(bf16[256,2048]{1,0:T(8,128)(2,1)} %get-tuple-element.5) | copy-start | bytes 3145732
where the time goes:
time: 181 us; the launch traced here: 180 us
  Pallas kernels  175 us (97%)
  local copies, waits for them, and re-layouts  4.91 us (3%)
    pallas_call x1, Pallas kernels, head_body(): pl.pallas_call(functools.partial(head_kernel, devices), out_shape=(slab,...  175 us

commit v1 on v0

--- a/solution.py
+++ b/solution.py
@@ -215,22 +215,18 @@
     return jnp.concatenate([high, low], axis=1)
 
 
-def attend_block(q_ref, k_ref, v_ref, out_ref, i, first, count, rows, banded):
-    scale = math.log2(math.e) / math.sqrt(q_ref.shape[1])
-    queries = q_ref[pl.ds(pl.multiple_of(i * rows, rows), rows), :]
-    base = pl.multiple_of(first * rows, rows)
-    row = lax.broadcasted_iota(jnp.int32, (rows, rows), 0)
-    col = lax.broadcasted_iota(jnp.int32, (rows, rows), 1)
+def score_blocks(queries, k_ref, base, count, rows, masks):
     scores, top = [], None
     for j in range(count):
         s = dot(queries, k_ref[pl.ds(base + j * rows, rows), :], NT)
-        if banded and j == 0:
-            s = jnp.where(row - col + (count - 1) * rows < WINDOW, s, masked_score)
-        if j == count - 1 or (not banded and j == count - 2):
-            s = jnp.where(row - col + (i - first - j) * rows >= 0, s, masked_score)
+        if masks[j] is not None:
+            s = jnp.where(masks[j], s, masked_score)
         scores.append(s)
         top = s if top is None else jnp.maximum(top, s)
-    top = jnp.max(top, axis=1, keepdims=True)
+    return scores, jnp.max(top, axis=1, keepdims=True)
+
+
+def weigh(scores, top, v_ref, base, rows, scale):
     total, weights = None, []
     for s in scores:
         w = jnp.exp2((s - top) * scale)
@@ -238,35 +234,51 @@
         weights.append(w.astype(BF16))
     total = jnp.sum(total, axis=1, keepdims=True)
     summed = dot(
-        jnp.concatenate(weights, axis=1), v_ref[pl.ds(base, count * rows), :]
-    )
-    out_ref[pl.ds(pl.multiple_of(i * rows, rows), rows), :] = (summed / total).astype(BF16)
-
-
-def attend_all(q_ref, k_ref, v_ref, out_ref, rows, order, done):
-    blocks = q_ref.shape[0] // rows
-    reach = WINDOW // rows
-    early = min(reach, blocks)
-
-    def one(t, carry):
-        i = order(t)
-        for low in range(0, early, 2):
-            high = min(low + 2, early)
-
-            @pl.when((i >= low) & (i < high))
-            def _(high=high):
-                attend_block(q_ref, k_ref, v_ref, out_ref, i, 0, high, rows, False)
-
-        if blocks > reach:
-
-            @pl.when(i >= reach)
-            def _():
-                attend_block(q_ref, k_ref, v_ref, out_ref, i, i - reach, reach + 1, rows, True)
-
-        done(i)
-        return carry
-
-    lax.fori_loop(0, blocks, one, 0)
+        jnp.concatenate(weights, axis=1), v_ref[pl.ds(base, len(scores) * rows), :]
+    )
+    return total, summed
+
+
+def index_gap(rows):
+    shape = (rows, rows)
+    return lax.broadcasted_iota(jnp.int32, shape, 0) - lax.broadcasted_iota(jnp.int32, shape, 1)
+
+
+def score_scale(size):
+    return math.log2(math.e) / math.sqrt(size)
+
+
+def block_of(i, rows):
+    return pl.ds(pl.multiple_of(i * rows, rows), rows)
+
+
+def attend_back(q_ref, k_ref, v_ref, o_ref, l_ref, i, low, count, rows):
+    size = q_ref.shape[1]
+    scale = score_scale(size)
+    gap = index_gap(rows)
+    masks = [gap + (i - low - j) * rows < 0 if j < 2 else None for j in range(count)]
+    queries = q_ref[block_of(i, rows), :]
+    scores, top = score_blocks(queries, k_ref, low * rows, count, rows, masks)
+    total, summed = weigh(scores, top, v_ref, low * rows, rows, scale)
+    o_ref[block_of(i, rows), :] = (summed / total).astype(BF16)
+    level = jnp.broadcast_to(top * scale + jnp.log2(total), (rows, size))
+    l_ref[i] = jnp.transpose(level)[:8, :]
+
+
+def attend_own(q_ref, k_ref, v_ref, o_ref, l_ref, out_ref, i, count, rows):
+    size = q_ref.shape[1]
+    scale = score_scale(size)
+    gap = index_gap(rows)
+    masks = [gap + (i - j) * rows >= 0 if j >= count - 2 else None for j in range(count)]
+    queries = q_ref[block_of(i, rows), :]
+    scores, top = score_blocks(queries, k_ref, 0, count, rows, masks)
+    total, summed = weigh(scores, top, v_ref, 0, rows, scale)
+    earlier = jnp.transpose(jnp.broadcast_to(l_ref[i][:1, :], (size, rows)))
+    level = top * scale
+    peak = jnp.maximum(earlier, level)
+    share_own, share_earlier = jnp.exp2(level - peak), jnp.exp2(earlier - peak)
+    joined = summed * share_own + o_ref[block_of(i, rows), :].astype(F32) * share_earlier
+    out_ref[block_of(i, rows), :] = (joined / (total * share_own + share_earlier)).astype(BF16)
 
 
 def flat(c, per):
@@ -310,7 +322,7 @@
     return mix, jnp.exp(col)
 
 
-def gram_states(k_ref, other_ref, rates_ref, starts_ref):
+def gram_states(k_ref, other_ref, rates_ref, first_ref, starts_ref, last_ref):
     per = rates_ref.shape[1] // 4
     chunks = rates_ref.shape[0] * per
 
@@ -321,7 +333,8 @@
             state = end * state + dot(keys, other_ref[span(c, per), :], TN)
         return state
 
-    lax.fori_loop(0, chunks // WAYS, step, jnp.zeros((CHUNK, CHUNK), F32))
+    last = lax.fori_loop(0, chunks // WAYS, step, first_ref[...].astype(F32))
+    last_ref[...] = last.astype(BF16)
 
 
 def solve_all(q_ref, k_ref, rates_ref, ridge_ref, gram_ref, x_ref):
@@ -382,111 +395,281 @@
         out_ref[span(c, per), :] = rows.astype(BF16)
 
 
-def head_kernel(n, *refs):
+KINDS = 13
+Q, K, V, MK, MQ, RATES, ATT, OUT, QX, PART, LEVEL, GRAM, CROSS = range(KINDS)
+
+
+def group_kernel(n, g, *refs):
     ins, rates_in, ridge_in = refs[:5], refs[5], refs[6]
     results = refs[7:9]
-    bufs, rates, homes = refs[9:14], refs[14], refs[15:17]
-    gram, cross, x = refs[17:20]
-    send, recv, own = refs[20:23]
+    bufs, qx, rates, homes = refs[9:14], refs[14], refs[15], refs[16:18]
+    o_out, o_in, l_out, l_in = refs[18:22]
+    g_first, g_last, c_first, c_last = refs[22:26]
+    gram, cross, x = refs[26:29]
+    send, recv, own = refs[29:32]
     q, k, v, mk, mq = bufs
     att, out = homes
     rows, size = ins[0].shape[0], ridge_in.shape[1]
+    per_device = rates.shape[0]
+    wide = per_device * size
+    groups = n // g
     group, me = lax.axis_index("groups"), lax.axis_index("seq")
+    sup, place = me // g, lax.rem(me, g)
 
     def row_block(ref, s):
         return ref.at[pl.ds(pl.multiple_of(s * rows, rows), rows), :]
 
-    def col_block(ref, h):
-        return ref.at[:, pl.ds(pl.multiple_of(h * size, size), size)]
-
-    def ends(a, source, target):
-        if a < 5:
-            return col_block(ins[a], target), row_block(bufs[a], source)
-        if a == 5:
-            return rates_in.at[target], rates.at[source]
-        return row_block(homes[a - 6], target), col_block(results[a - 6], source)
-
-    def remote(a, source, target, peer):
-        src, dst = ends(a, source, target)
+    def head_col(ref, j):
+        return ref.at[:, pl.ds(pl.multiple_of(j * size, size), size)]
+
+    def cell(ref, s, j):
+        return ref.at[
+            pl.ds(pl.multiple_of(s * rows, rows), rows),
+            pl.ds(pl.multiple_of(j * size, size), size),
+        ]
+
+    def ends(a, j, source, target):
+        if a in (MK, MQ):
+            src = ins[a].at[:, pl.ds(pl.multiple_of(target * wide, wide), wide)]
+            return src, row_block(bufs[a], source)
+        if a in (Q, K, V):
+            return head_col(ins[a], target * per_device + j), cell(bufs[a], source, j)
+        if a == QX:
+            return head_col(ins[Q], target * per_device + j), cell(qx, source, j)
+        if a == RATES:
+            return rates_in.at[pl.ds(target * per_device, per_device)], rates.at[:, source]
+        return cell(homes[a - ATT], target, j), head_col(results[a - ATT], source * per_device + j)
+
+    def copy_to(src, dst, a, j, sent, got, peer):
         return pltpu.make_async_remote_copy(
             src_ref=src,
             dst_ref=dst,
-            send_sem=send.at[a, target],
-            recv_sem=recv.at[a, source],
+            send_sem=send.at[a, j, sent],
+            recv_sem=recv.at[a, j, got],
             device_id=(group, peer),
             device_id_type=pl.DeviceIdType.MESH,
         )
 
-    def local(a):
-        src, dst = ends(a, me, me)
-        return pltpu.make_async_copy(src, dst, own.at[a])
-
-    def other(t):
-        return lax.rem(me + t, n)
-
-    def over_peers(act):
+    def remote(a, j, source, target, peer):
+        src, dst = ends(a, j, source, target)
+        return copy_to(src, dst, a, j, target, source, peer)
+
+    def local(a, j):
+        src, dst = ends(a, j, place, place)
+        return pltpu.make_async_copy(src, dst, own.at[a, j])
+
+    def onward(a, j, i):
+        if a == PART:
+            src, dst = cell(o_out, i, j), cell(o_in, i, j)
+        elif a == LEVEL:
+            src, dst = l_out.at[j, i], l_in.at[j, i]
+        elif a == GRAM:
+            src, dst = g_last.at[j], g_first.at[j]
+        else:
+            src, dst = c_last.at[j], c_first.at[j]
+        return copy_to(src, dst, a, j, i, i, me + g)
+
+    has_next, has_previous = sup + 1 < groups, sup > 0
+
+    def loop(first, last, act):
         def one(t, carry):
-            act(other(t))
+            act(t)
             return carry
 
-        lax.fori_loop(1, n, one, 0)
-
-    def arrive(a):
-        over_peers(lambda peer: remote(a, peer, me, peer).wait_recv())
-        local(a).wait()
-
-    def give(a, slab):
-        @pl.when(slab != me)
-        def _():
-            remote(a, me, slab, slab).start()
-
-        @pl.when(slab == me)
-        def _():
-            local(a).start()
-
-    barrier = pltpu.get_barrier_semaphore()
-    over_peers(
-        lambda peer: pl.semaphore_signal(
+        lax.fori_loop(first, last, one, 0)
+
+    def others(act):
+        loop(1, g, lambda t: act(lax.rem(place + t, g)))
+
+    def signal(peer):
+        pl.semaphore_signal(
             barrier, inc=1, device_id=(group, peer), device_id_type=pl.DeviceIdType.MESH
         )
-    )
-    pl.semaphore_wait(barrier, n - 1)
-    for a in SEND_ORDER:
-        over_peers(lambda peer: remote(a, me, peer, peer).start())
-        local(a).start()
-
-    for a in (5, 3, 4):
-        arrive(a)
-    gram_states(mk, mk, rates, gram)
-    solve_all(mq, mk, rates, ridge_in[pl.ds(me, 1), :], gram, x)
-    for a in (0, 1, 2):
-        arrive(a)
-    attend_all(q, k, v, att, rows, lambda t: other(t + 1), lambda i: give(6, i))
-    gram_states(mk, att, rates, cross)
-
-    def slab_out(t, carry):
-        slab = other(t + 1)
-        read_out(mk, att, rates, cross, x, out, slab)
-        give(7, slab)
-        return carry
-
-    lax.fori_loop(0, n, slab_out, 0)
-    for a in (6, 7):
-        arrive(a)
-    for a in range(8):
-        over_peers(lambda peer: remote(a, me, peer, peer).wait_send())
-
-
-SEND_ORDER = (5, 3, 4, 0, 1, 2)
-
-
-def head_body(
+
+    def home(e):
+        return sup * g + e
+
+    def push(a, j):
+        others(lambda e: remote(a, j, place, e, home(e)).start())
+        local(a, j).start()
+
+    def arrive(a, j):
+        others(lambda e: remote(a, j, e, place, home(e)).wait_recv())
+        local(a, j).wait()
+
+    def give(a, j, e):
+        @pl.when(e != place)
+        def _():
+            remote(a, j, place, e, home(e)).start()
+
+        @pl.when(e == place)
+        def _():
+            local(a, j).start()
+
+    barrier = pltpu.get_barrier_semaphore()
+    others(lambda e: signal(home(e)))
+
+    @pl.when(has_previous)
+    def _():
+        loop(0, g, lambda e: signal(home(e) - g))
+
+    @pl.when(has_next)
+    def _():
+        loop(0, g, lambda e: signal(home(e) + g))
+
+    near = has_previous.astype(jnp.int32) + has_next.astype(jnp.int32)
+    pl.semaphore_wait(barrier, g - 1 + g * near)
+
+    for a in (RATES, MK, MQ):
+        push(a, 0)
+
+    def push_head(j):
+        push(K, j)
+        push(V, j)
+
+        @pl.when(has_previous)
+        def _():
+            def one(t):
+                e = lax.rem(place + t, g)
+                remote(QX, j, place, e, home(e) - g).start()
+
+            loop(0, g, one)
+
+        push(Q, j)
+
+    loop(0, per_device, push_head)
+
+    @pl.when(jnp.logical_not(has_previous))
+    def _():
+        g_first[...] = jnp.zeros_like(g_first)
+        c_first[...] = jnp.zeros_like(c_first)
+        o_in[...] = jnp.zeros_like(o_in)
+        l_in[...] = jnp.full_like(l_in, masked_score)
+
+    arrive(RATES, 0)
+    arrive(MK, 0)
+
+    def gram_head(j):
+        @pl.when(has_previous)
+        def _():
+            onward(GRAM, j, 0).wait_recv()
+
+        keys = head_col(mk, j)
+        gram_states(keys, keys, rates.at[j], g_first.at[j], gram.at[j], g_last.at[j])
+
+        @pl.when(has_next)
+        def _():
+            onward(GRAM, j, 0).start()
+
+    loop(0, per_device, gram_head)
+    arrive(MQ, 0)
+
+    def solve_head(j):
+        ridge = ridge_in[pl.ds(place * per_device + j, 1), :]
+        solve_all(head_col(mq, j), head_col(mk, j), rates.at[j], ridge, gram.at[j], head_col(x, j))
+
+    loop(0, per_device, solve_head)
+
+    def attend_head(j):
+        queries, keys, values = head_col(q, j), head_col(k, j), head_col(v, j)
+        arrive(K, j)
+        arrive(V, j)
+
+        @pl.when(has_next)
+        def _():
+            def one(i):
+                remote(QX, j, i, place, home(i) + g).wait_recv()
+                for low in range(0, g, 2):
+
+                    @pl.when((i >= low) & (i < low + 2))
+                    def _(low=low):
+                        attend_back(
+                            head_col(qx, j), keys, values, head_col(o_out, j), l_out.at[j],
+                            i, low, g - low, rows,
+                        )
+
+                onward(PART, j, i).start()
+                onward(LEVEL, j, i).start()
+
+            loop(0, g, one)
+
+        arrive(Q, j)
+
+        def one(i):
+            @pl.when(has_previous)
+            def _():
+                onward(PART, j, i).wait_recv()
+                onward(LEVEL, j, i).wait_recv()
+
+            for low in range(0, g, 2):
+
+                @pl.when((i >= low) & (i < low + 2))
+                def _(low=low):
+                    attend_own(
+                        queries, keys, values, head_col(o_in, j), l_in.at[j], head_col(att, j),
+                        i, low + 2, rows,
+                    )
+
+            give(ATT, j, i)
+
+        loop(0, g, one)
+
+        @pl.when(has_previous)
+        def _():
+            onward(CROSS, j, 0).wait_recv()
+
+        gram_states(
+            head_col(mk, j), head_col(att, j), rates.at[j], c_first.at[j], cross.at[j], c_last.at[j]
+        )
+
+        @pl.when(has_next)
+        def _():
+            onward(CROSS, j, 0).start()
+
+        def slab_out(i):
+            read_out(
+                head_col(mk, j), head_col(att, j), rates.at[j], cross.at[j], head_col(x, j),
+                head_col(out, j), i,
+            )
+            give(OUT, j, i)
+
+        loop(0, g, slab_out)
+
+    loop(0, per_device, attend_head)
+
+    def finish(j):
+        for a in (ATT, OUT):
+            arrive(a, j)
+        for a in (Q, K, V, ATT, OUT):
+            others(lambda e: remote(a, j, place, e, home(e)).wait_send())
+
+        @pl.when(has_previous)
+        def _():
+            loop(0, g, lambda e: remote(QX, j, place, e, home(e) - g).wait_send())
+
+        @pl.when(has_next)
+        def _():
+            def one(i):
+                onward(PART, j, i).wait_send()
+                onward(LEVEL, j, i).wait_send()
+
+            loop(0, g, one)
+            onward(GRAM, j, 0).wait_send()
+            onward(CROSS, j, 0).wait_send()
+
+    loop(0, per_device, finish)
+    for a in (RATES, MK, MQ):
+        others(lambda e: remote(a, 0, place, e, home(e)).wait_send())
+
+
+def group_body(
     attn_query, attn_key, attn_value, mesa_query, mesa_key, log_decay, input_gate, regularizer
 ):
     rows = attn_query.shape[0]
     heads, size = regularizer.shape
     devices = lax.axis_size("seq")
-    tokens = rows * devices
+    g = WINDOW // rows
+    per_device, tokens = heads // g, WINDOW
     per, chunks = rows // CHUNK, tokens // CHUNK
     cum = jnp.cumsum(log_decay.reshape(per, CHUNK, heads), axis=1)
     rates = jnp.concatenate([cum, input_gate.reshape(per, CHUNK, heads)], axis=0)
@@ -494,20 +677,26 @@
     slab = jax.ShapeDtypeStruct((rows, heads * size), BF16)
     vmem = pl.BlockSpec(memory_space=pltpu.VMEM)
     anywhere = pl.BlockSpec(memory_space=pl.ANY)
+    tall = pltpu.VMEM((tokens, per_device * size), BF16)
+    levels = pltpu.VMEM((per_device, g, 8, rows), F32)
+    state = pltpu.VMEM((per_device, size, size), BF16)
+    states = pltpu.VMEM((per_device, chunks, size, size), BF16)
     return pl.pallas_call(
-        functools.partial(head_kernel, devices),
+        functools.partial(group_kernel, devices, g),
         out_shape=(slab, slab),
         in_specs=[anywhere] * 5 + [vmem] * 2,
         out_specs=(anywhere, anywhere),
-        scratch_shapes=[pltpu.VMEM((tokens, size), BF16)] * 5
-        + [pltpu.VMEM((devices, 4 * per, CHUNK), F32)]
-        + [pltpu.VMEM((tokens, size), BF16)] * 2
-        + [pltpu.VMEM((chunks, size, size), BF16)] * 2
+        scratch_shapes=[tall] * 6
+        + [pltpu.VMEM((per_device, g, 4 * per, CHUNK), F32)]
+        + [tall] * 4
+        + [levels] * 2
+        + [state] * 4
+        + [states] * 2
         + [
-            pltpu.VMEM((tokens, size), F32),
-            pltpu.SemaphoreType.DMA((8, devices)),
-            pltpu.SemaphoreType.DMA((8, devices)),
-            pltpu.SemaphoreType.DMA((8,)),
+            pltpu.VMEM((tokens, per_device * size), F32),
+            pltpu.SemaphoreType.DMA((KINDS, per_device, g)),
+            pltpu.SemaphoreType.DMA((KINDS, per_device, g)),
+            pltpu.SemaphoreType.DMA((KINDS, per_device)),
         ],
         compiler_params=pltpu.CompilerParams(
             collective_id=0, has_side_effects=True, vmem_limit_bytes=56 * 1024 * 1024
@@ -515,15 +704,17 @@
     )(attn_query, attn_key, attn_value, mesa_key, mesa_query, rates, regularizer)
 
 
-def fits_heads(mesh, rows, heads, size):
-    tokens = rows * mesh.shape["seq"]
+def fits_groups(mesh, rows, heads, size):
+    g = WINDOW // rows
     return (
-        mesh.shape["seq"] == heads
-        and size == CHUNK
+        size == CHUNK
         and WINDOW % rows == 0
+        and g % 2 == 0
+        and mesh.shape["seq"] % g == 0
+        and heads % g == 0
         and rows % CHUNK == 0
         and WAYS % (rows // CHUNK) == 0
-        and tokens % (CHUNK * WAYS) == 0
+        and WINDOW % (CHUNK * WAYS) == 0
     )
 
 
@@ -532,8 +723,8 @@
 
     def body(*args):
         heads, size = args[7].shape
-        chosen = head_body if fits_heads(mesh, args[0].shape[0], heads, size) else slab_body
-        return chosen(*args)
+        fits = fits_groups(mesh, args[0].shape[0], heads, size)
+        return (group_body if fits else slab_body)(*args)
 
     return jax.shard_map(
         body,

time: 181 us -> 171 us (0.945)
  Pallas kernels: 175 us -> 165 us
    pallas_call x1, Pallas kernels: 175 us -> 165 us  [group_body(): pl.pallas_call(functools.partial(group_kernel, devices, g), out_shape=(sl...]
where the time goes in v1:
time: 171 us
  Pallas kernels  165 us (96%)
  local copies, waits for them, and re-layouts  4.91 us (3%)
    pallas_call x1, Pallas kernels, group_body(): pl.pallas_call(functools.partial(group_kernel, devices, g), out_shape=(sl...  165 us

profile of v1, /device:TPU:29, one launch (start us, length us, event | category | flops | bytes accessed | tf_op | source)
XLA Modules:
  0.0 171.0 jit_solution(8023743849151839788)
XLA Ops:
  0.6 0.0 copy-start.1
  0.6 0.7 reshape.11
  1.4 0.0 copy-done.1
  1.4 0.1 copy.12
  1.5 0.2 reduce_window_sum.11
  1.7 0.1 copy.11
  1.8 0.6 pad.4.refs_5_
  2.4 165.2 %shard_map.95 = (bf16[256,2048]{1,0:T(8,128)(2,1)}, bf16[256,2048]{1,0:T(8,128)(2,1)}) custom-call(bf16[256,2048]{1,0:T(8,128)(2,1)} %refs_0_.1, bf16[256,2048]{1,0:T(8,128)(2,1)} %refs_1_.1, bf16[256,2048]{1,0:T(8,128)(2,1)} %refs_2_.1, bf16[256,2048]{1,0:T(8,128)(2,1)} %refs_3_.1, bf16[256,2048]{1,0:T(8,128)(2,1)} %refs_4_.1, f32[16,8,128]{2,1,0:T(8,128)} %pad.4.refs_5_, ...), custom_call_target="tpu_custom_call" | custom-call | tf_op jit(solution)/shard_map/pallas_call | solution.py:684
  167.6 0.0 copy-start
  167.6 2.4 %copy.15 = bf16[256,2048]{1,0:T(8,128)(2,1)} copy(bf16[256,2048]{1,0:T(8,128)(2,1)} %get-tuple-element.4) | data formatting | bytes 2097152
  170.0 0.0 copy-done
  170.0 1.0 copy.16
  (1 shorter events, 0.0 us)
Async XLA Ops:
  0.6 0.7 copy-start.1
  167.6 2.4 %copy-start = (bf16[256,2048]{1,0:T(8,128)(2,1)S(1)}, bf16[256,2048]{1,0:T(8,128)(2,1)}, u32[]{:S(2)}) copy-start(bf16[256,2048]{1,0:T(8,128)(2,1)} %get-tuple-element.5) | copy-start | bytes 3145732

commit v2 on v1

--- a/solution.py
+++ b/solution.py
@@ -244,41 +244,63 @@
     return lax.broadcasted_iota(jnp.int32, shape, 0) - lax.broadcasted_iota(jnp.int32, shape, 1)
 
 
-def score_scale(size):
-    return math.log2(math.e) / math.sqrt(size)
-
-
 def block_of(i, rows):
+    if isinstance(i, int):
+        return pl.ds(i * rows, rows)
     return pl.ds(pl.multiple_of(i * rows, rows), rows)
 
 
-def attend_back(q_ref, k_ref, v_ref, o_ref, l_ref, i, low, count, rows):
-    size = q_ref.shape[1]
-    scale = score_scale(size)
-    gap = index_gap(rows)
-    masks = [gap + (i - low - j) * rows < 0 if j < 2 else None for j in range(count)]
+def partial(q_ref, k_ref, v_ref, i, base, masks, rows):
+    scale = math.log2(math.e) / math.sqrt(q_ref.shape[1])
     queries = q_ref[block_of(i, rows), :]
-    scores, top = score_blocks(queries, k_ref, low * rows, count, rows, masks)
-    total, summed = weigh(scores, top, v_ref, low * rows, rows, scale)
-    o_ref[block_of(i, rows), :] = (summed / total).astype(BF16)
-    level = jnp.broadcast_to(top * scale + jnp.log2(total), (rows, size))
-    l_ref[i] = jnp.transpose(level)[:8, :]
-
-
-def attend_own(q_ref, k_ref, v_ref, o_ref, l_ref, out_ref, i, count, rows):
-    size = q_ref.shape[1]
-    scale = score_scale(size)
-    gap = index_gap(rows)
-    masks = [gap + (i - j) * rows >= 0 if j >= count - 2 else None for j in range(count)]
-    queries = q_ref[block_of(i, rows), :]
-    scores, top = score_blocks(queries, k_ref, 0, count, rows, masks)
-    total, summed = weigh(scores, top, v_ref, 0, rows, scale)
-    earlier = jnp.transpose(jnp.broadcast_to(l_ref[i][:1, :], (size, rows)))
-    level = top * scale
+    scores, top = score_blocks(queries, k_ref, base, len(masks), rows, masks)
+    total, summed = weigh(scores, top, v_ref, base, rows, scale)
+    return top * scale, total, summed
+
+
+def joined(part, o_ref, l_ref, i, rows):
+    level, total, summed = part
+    earlier = jnp.transpose(jnp.broadcast_to(l_ref[i][:1, :], (summed.shape[1], rows)))
     peak = jnp.maximum(earlier, level)
     share_own, share_earlier = jnp.exp2(level - peak), jnp.exp2(earlier - peak)
-    joined = summed * share_own + o_ref[block_of(i, rows), :].astype(F32) * share_earlier
-    out_ref[block_of(i, rows), :] = (joined / (total * share_own + share_earlier)).astype(BF16)
+    summed = summed * share_own + o_ref[block_of(i, rows), :].astype(F32) * share_earlier
+    return peak, total * share_own + share_earlier, summed
+
+
+def store_part(part, o_ref, l_ref, i, rows):
+    level, total, summed = part
+    o_ref[block_of(i, rows), :] = (summed / total).astype(BF16)
+    level = jnp.broadcast_to(level + jnp.log2(total), summed.shape)
+    l_ref[i] = jnp.transpose(level)[:8, :]
+
+
+def attend_far(q_ref, k_ref, v_ref, o_ref, l_ref, rows):
+    blocks = k_ref.shape[0] // rows
+    beyond = index_gap(rows) < 0
+    for i in range(blocks):
+        masks = [beyond] + [None] * (blocks - i - 1)
+        store_part(partial(q_ref, k_ref, v_ref, i, i * rows, masks, rows), o_ref, l_ref, i, rows)
+
+
+def attend_middle(q_ref, k_ref, v_ref, o_in, l_in, o_ref, l_ref, rows):
+    blocks = k_ref.shape[0] // rows
+
+    def one(i, carry):
+        part = partial(q_ref, k_ref, v_ref, i, 0, [None] * blocks, rows)
+        store_part(joined(part, o_in, l_in, i, rows), o_ref, l_ref, i, rows)
+        return carry
+
+    lax.fori_loop(0, blocks, one, 0)
+
+
+def attend_own(q_ref, k_ref, v_ref, o_in, l_in, out_ref, rows, done):
+    blocks = k_ref.shape[0] // rows
+    causal = index_gap(rows) >= 0
+    for i in range(blocks):
+        part = partial(q_ref, k_ref, v_ref, i, 0, [None] * i + [causal], rows)
+        level, total, summed = joined(part, o_in, l_in, i, rows)
+        out_ref[block_of(i, rows), :] = (summed / total).astype(BF16)
+        done(i)
 
 
 def flat(c, per):
@@ -322,19 +344,43 @@
     return mix, jnp.exp(col)
 
 
-def gram_states(k_ref, other_ref, rates_ref, first_ref, starts_ref, last_ref):
+def state_totals(k_ref, other_ref, rates_ref, zero_ref, total_ref):
     per = rates_ref.shape[1] // 4
     chunks = rates_ref.shape[0] * per
 
-    def step(g, state):
+    def step(g, carry):
+        state, decay = carry
         for c in chunk_ids(g, per):
-            starts_ref[flat(c, per)] = state.astype(BF16)
+            zero_ref[flat(c, per)] = state
             keys, end = tail_keys(k_ref, rates_ref, c, per)
             state = end * state + dot(keys, other_ref[span(c, per), :], TN)
-        return state
-
-    last = lax.fori_loop(0, chunks // WAYS, step, first_ref[...].astype(F32))
-    last_ref[...] = last.astype(BF16)
+            decay = decay * end
+        return state, decay
+
+    state, decay = lax.fori_loop(
+        0, chunks // WAYS, step, (jnp.zeros((CHUNK, CHUNK), F32), jnp.ones((1, 1), F32))
+    )
+    total_ref[...] = state.astype(BF16)
+    return decay
+
+
+def state_starts(rates_ref, zero_ref, totals_ref, decay_ref, count, starts_ref):
+    per = rates_ref.shape[1] // 4
+    chunks = rates_ref.shape[0] * per
+
+    def plane(p, first):
+        return decay_ref(p) * first + totals_ref[p].astype(F32)
+
+    first = lax.fori_loop(0, count, plane, jnp.zeros((CHUNK, CHUNK), F32))
+
+    def step(g, first):
+        for c in chunk_ids(g, per):
+            starts_ref[flat(c, per)] = (zero_ref[flat(c, per)] + first).astype(BF16)
+            cum, gate = rates_of(rates_ref, c)
+            first = first * jnp.exp(cum[:, CHUNK - 1 :])
+        return first
+
+    lax.fori_loop(0, chunks // WAYS, step, first)
 
 
 def solve_all(q_ref, k_ref, rates_ref, ridge_ref, gram_ref, x_ref):
@@ -395,26 +441,31 @@
         out_ref[span(c, per), :] = rows.astype(BF16)
 
 
-KINDS = 13
-Q, K, V, MK, MQ, RATES, ATT, OUT, QX, PART, LEVEL, GRAM, CROSS = range(KINDS)
-
-
-def group_kernel(n, g, *refs):
+REACH = 2
+Q, K, V, MK, MQ, RATES, ATT, OUT, GRAM, CROSS, DECAY = range(11)
+QX, PART, LEVEL = (11, 13, 15)
+KINDS = 17
+
+
+def plane_kernel(n, g, *refs):
     ins, rates_in, ridge_in = refs[:5], refs[5], refs[6]
     results = refs[7:9]
-    bufs, qx, rates, homes = refs[9:14], refs[14], refs[15], refs[16:18]
-    o_out, o_in, l_out, l_in = refs[18:22]
-    g_first, g_last, c_first, c_last = refs[22:26]
-    gram, cross, x = refs[26:29]
-    send, recv, own = refs[29:32]
+    bufs, rates, homes = refs[9:14], refs[14], refs[15:17]
+    later = (refs[9],) + refs[17:19]
+    o_out, o_in = (None,) + refs[19:21], (None,) + refs[21:23]
+    l_out, l_in = (None,) + refs[23:25], (None,) + refs[25:27]
+    total_out, total_in = {GRAM: refs[27], CROSS: refs[28]}, {GRAM: refs[29], CROSS: refs[30]}
+    decay_out, decay_in, zero = refs[31:34]
+    gram, cross, x = refs[34:37]
+    send, recv, own = refs[37:40]
     q, k, v, mk, mq = bufs
     att, out = homes
     rows, size = ins[0].shape[0], ridge_in.shape[1]
     per_device = rates.shape[0]
     wide = per_device * size
-    groups = n // g
+    planes = n // g
     group, me = lax.axis_index("groups"), lax.axis_index("seq")
-    sup, place = me // g, lax.rem(me, g)
+    plane, place = me // g, lax.rem(me, g)
 
     def row_block(ref, s):
         return ref.at[pl.ds(pl.multiple_of(s * rows, rows), rows), :]
@@ -434,8 +485,6 @@
             return src, row_block(bufs[a], source)
         if a in (Q, K, V):
             return head_col(ins[a], target * per_device + j), cell(bufs[a], source, j)
-        if a == QX:
-            return head_col(ins[Q], target * per_device + j), cell(qx, source, j)
         if a == RATES:
             return rates_in.at[pl.ds(target * per_device, per_device)], rates.at[:, source]
         return cell(homes[a - ATT], target, j), head_col(results[a - ATT], source * per_device + j)
@@ -450,26 +499,35 @@
             device_id_type=pl.DeviceIdType.MESH,
         )
 
+    def home(e):
+        return plane * g + e
+
     def remote(a, j, source, target, peer):
         src, dst = ends(a, j, source, target)
-        return copy_to(src, dst, a, j, target, source, peer)
+        return copy_to(src, dst, a, j, target, source, home(peer))
 
     def local(a, j):
         src, dst = ends(a, j, place, place)
         return pltpu.make_async_copy(src, dst, own.at[a, j])
 
-    def onward(a, j, i):
+    def back(d, j):
+        return copy_to(
+            head_col(later[d - 1], j), head_col(later[d], j), QX + d - 1, j, 0, 0, me - g
+        )
+
+    def onward(a, d, j):
         if a == PART:
-            src, dst = cell(o_out, i, j), cell(o_in, i, j)
-        elif a == LEVEL:
-            src, dst = l_out.at[j, i], l_in.at[j, i]
-        elif a == GRAM:
-            src, dst = g_last.at[j], g_first.at[j]
+            src, dst = head_col(o_out[d], j), head_col(o_in[d], j)
         else:
-            src, dst = c_last.at[j], c_first.at[j]
-        return copy_to(src, dst, a, j, i, i, me + g)
-
-    has_next, has_previous = sup + 1 < groups, sup > 0
+            src, dst = l_out[d].at[j], l_in[d].at[j]
+        return copy_to(src, dst, a + d - 1, j, 0, 0, me + g)
+
+    def state(a, j, source, target, peer_plane):
+        if a == DECAY:
+            src, dst = decay_out, decay_in.at[source]
+        else:
+            src, dst = total_out[a].at[j], total_in[a].at[j, source]
+        return copy_to(src, dst, a, j, target, source, peer_plane * g + place)
 
     def loop(first, last, act):
         def one(t, carry):
@@ -481,195 +539,228 @@
     def others(act):
         loop(1, g, lambda t: act(lax.rem(place + t, g)))
 
+    def later_planes(act):
+        loop(plane + 1, planes, act)
+
     def signal(peer):
         pl.semaphore_signal(
             barrier, inc=1, device_id=(group, peer), device_id_type=pl.DeviceIdType.MESH
         )
 
-    def home(e):
-        return sup * g + e
-
     def push(a, j):
-        others(lambda e: remote(a, j, place, e, home(e)).start())
+        others(lambda e: remote(a, j, place, e, e).start())
         local(a, j).start()
 
     def arrive(a, j):
-        others(lambda e: remote(a, j, e, place, home(e)).wait_recv())
+        others(lambda e: remote(a, j, e, place, e).wait_recv())
         local(a, j).wait()
 
     def give(a, j, e):
         @pl.when(e != place)
         def _():
-            remote(a, j, place, e, home(e)).start()
+            remote(a, j, place, e, e).start()
 
         @pl.when(e == place)
         def _():
             local(a, j).start()
 
+    def reaches(d):
+        return plane + d < planes
+
+    has_previous = plane > 0
+
     barrier = pltpu.get_barrier_semaphore()
     others(lambda e: signal(home(e)))
-
-    @pl.when(has_previous)
+    loop(1, planes, lambda t: signal(lax.rem(plane + t, planes) * g + place))
+    pl.semaphore_wait(barrier, g - 1 + planes - 1)
+
+    push(RATES, 0)
+    for j in range(per_device):
+        push(Q, j)
+
+    @pl.when(jnp.logical_not(has_previous))
     def _():
-        loop(0, g, lambda e: signal(home(e) - g))
-
-    @pl.when(has_next)
-    def _():
-        loop(0, g, lambda e: signal(home(e) + g))
-
-    near = has_previous.astype(jnp.int32) + has_next.astype(jnp.int32)
-    pl.semaphore_wait(barrier, g - 1 + g * near)
-
-    for a in (RATES, MK, MQ):
-        push(a, 0)
-
-    def push_head(j):
+        for d in range(1, REACH + 1):
+            o_in[d][...] = jnp.zeros_like(o_in[d])
+            l_in[d][...] = jnp.full_like(l_in[d], masked_score)
+
+    def forward(j):
+        arrive(Q, j)
+
+        @pl.when(has_previous)
+        def _():
+            back(1, j).start()
+
+    def relay(j):
+        @pl.when(reaches(1))
+        def _():
+            back(1, j).wait_recv()
+
+            @pl.when(has_previous)
+            def _():
+                back(2, j).start()
+
+    def push_values(j):
         push(K, j)
         push(V, j)
 
-        @pl.when(has_previous)
-        def _():
-            def one(t):
-                e = lax.rem(place + t, g)
-                remote(QX, j, place, e, home(e) - g).start()
-
-            loop(0, g, one)
-
-        push(Q, j)
-
-    loop(0, per_device, push_head)
-
-    @pl.when(jnp.logical_not(has_previous))
-    def _():
-        g_first[...] = jnp.zeros_like(g_first)
-        c_first[...] = jnp.zeros_like(c_first)
-        o_in[...] = jnp.zeros_like(o_in)
-        l_in[...] = jnp.full_like(l_in, masked_score)
-
+    for j in range(per_device):
+        forward(j)
+        if j == 0:
+            push(MK, 0)
+            push_values(0)
+        if j > 0:
+            relay(j - 1)
+    push(MQ, 0)
+    push_values(1)
     arrive(RATES, 0)
     arrive(MK, 0)
 
+    def head_totals(a, j, others_ref):
+        decay = state_totals(
+            head_col(mk, j), head_col(others_ref, j), rates.at[j], zero.at[a - GRAM, j],
+            total_out[a].at[j],
+        )
+        later_planes(lambda p: state(a, j, plane, p, p).start())
+        return decay
+
+    def head_starts(a, j, starts_ref):
+        loop(0, plane, lambda p: state(a, j, p, plane, p).wait_recv())
+        state_starts(
+            rates.at[j], zero.at[a - GRAM, j], total_in[a].at[j],
+            lambda p: decay_in[p, pl.ds(j, 1), :], plane, starts_ref.at[j],
+        )
+
     def gram_head(j):
-        @pl.when(has_previous)
+        decay = head_totals(GRAM, j, mk)
+        decay_out[pl.ds(j, 1), :] = jnp.broadcast_to(decay, (1, size))
+
+    loop(0, per_device, gram_head)
+    later_planes(lambda p: state(DECAY, 0, plane, p, p).start())
+    relay(per_device - 1)
+
+    def step(s):
+        far, middle, near, last = s, s - 1, s - 2, s - 3
+
+        @pl.when(far < per_device)
         def _():
-            onward(GRAM, j, 0).wait_recv()
-
-        keys = head_col(mk, j)
-        gram_states(keys, keys, rates.at[j], g_first.at[j], gram.at[j], g_last.at[j])
-
-        @pl.when(has_next)
+            j = far
+            arrive(K, j)
+            arrive(V, j)
+
+            @pl.when(j + 2 < per_device)
+            def _():
+                push_values(j + 2)
+
+            @pl.when(reaches(2))
+            def _():
+                back(2, j).wait_recv()
+                attend_far(
+                    head_col(later[2], j), head_col(k, j), head_col(v, j),
+                    head_col(o_out[2], j), l_out[2].at[j], rows,
+                )
+                onward(PART, 2, j).start()
+                onward(LEVEL, 2, j).start()
+
+        @pl.when((middle >= 0) & (middle < per_device))
         def _():
-            onward(GRAM, j, 0).start()
-
-    loop(0, per_device, gram_head)
-    arrive(MQ, 0)
-
-    def solve_head(j):
-        ridge = ridge_in[pl.ds(place * per_device + j, 1), :]
-        solve_all(head_col(mq, j), head_col(mk, j), rates.at[j], ridge, gram.at[j], head_col(x, j))
-
-    loop(0, per_device, solve_head)
-
-    def attend_head(j):
-        queries, keys, values = head_col(q, j), head_col(k, j), head_col(v, j)
-        arrive(K, j)
-        arrive(V, j)
-
-        @pl.when(has_next)
+            j = middle
+
+            @pl.when(reaches(1))
+            def _():
+                @pl.when(has_previous)
+                def _():
+                    onward(PART, 2, j).wait_recv()
+                    onward(LEVEL, 2, j).wait_recv()
+
+                attend_middle(
+                    head_col(later[1], j), head_col(k, j), head_col(v, j),
+                    head_col(o_in[2], j), l_in[2].at[j],
+                    head_col(o_out[1], j), l_out[1].at[j], rows,
+                )
+                onward(PART, 1, j).start()
+                onward(LEVEL, 1, j).start()
+
+            @pl.when(j == 0)
+            def _():
+                arrive(MQ, 0)
+                loop(0, plane, lambda p: state(DECAY, 0, p, plane, p).wait_recv())
+
+            head_starts(GRAM, j, gram)
+            solve_all(
+                head_col(mq, j), head_col(mk, j), rates.at[j],
+                ridge_in[pl.ds(place * per_device + j, 1), :], gram.at[j], head_col(x, j),
+            )
+
+        @pl.when((near >= 0) & (near < per_device))
         def _():
-            def one(i):
-                remote(QX, j, i, place, home(i) + g).wait_recv()
-                for low in range(0, g, 2):
-
-                    @pl.when((i >= low) & (i < low + 2))
-                    def _(low=low):
-                        attend_back(
-                            head_col(qx, j), keys, values, head_col(o_out, j), l_out.at[j],
-                            i, low, g - low, rows,
-                        )
-
-                onward(PART, j, i).start()
-                onward(LEVEL, j, i).start()
-
-            loop(0, g, one)
-
-        arrive(Q, j)
-
-        def one(i):
+            j = near
+
             @pl.when(has_previous)
             def _():
-                onward(PART, j, i).wait_recv()
-                onward(LEVEL, j, i).wait_recv()
-
-            for low in range(0, g, 2):
-
-                @pl.when((i >= low) & (i < low + 2))
-                def _(low=low):
-                    attend_own(
-                        queries, keys, values, head_col(o_in, j), l_in.at[j], head_col(att, j),
-                        i, low + 2, rows,
-                    )
-
-            give(ATT, j, i)
-
-        loop(0, g, one)
-
-        @pl.when(has_previous)
+                onward(PART, 1, j).wait_recv()
+                onward(LEVEL, 1, j).wait_recv()
+
+            attend_own(
+                head_col(q, j), head_col(k, j), head_col(v, j), head_col(o_in[1], j),
+                l_in[1].at[j], head_col(att, j), rows, lambda i: give(ATT, j, i),
+            )
+            head_totals(CROSS, j, att)
+
+        @pl.when(last >= 0)
         def _():
-            onward(CROSS, j, 0).wait_recv()
-
-        gram_states(
-            head_col(mk, j), head_col(att, j), rates.at[j], c_first.at[j], cross.at[j], c_last.at[j]
-        )
-
-        @pl.when(has_next)
-        def _():
-            onward(CROSS, j, 0).start()
-
-        def slab_out(i):
-            read_out(
-                head_col(mk, j), head_col(att, j), rates.at[j], cross.at[j], head_col(x, j),
-                head_col(out, j), i,
-            )
-            give(OUT, j, i)
-
-        loop(0, g, slab_out)
-
-    loop(0, per_device, attend_head)
+            j = last
+            head_starts(CROSS, j, cross)
+
+            def slab_out(i):
+                read_out(
+                    head_col(mk, j), head_col(att, j), rates.at[j], cross.at[j], head_col(x, j),
+                    head_col(out, j), i,
+                )
+                give(OUT, j, i)
+
+            loop(0, g, slab_out)
+
+    loop(0, per_device + 3, step)
 
     def finish(j):
         for a in (ATT, OUT):
             arrive(a, j)
         for a in (Q, K, V, ATT, OUT):
-            others(lambda e: remote(a, j, place, e, home(e)).wait_send())
+            others(lambda e: remote(a, j, place, e, e).wait_send())
 
         @pl.when(has_previous)
         def _():
-            loop(0, g, lambda e: remote(QX, j, place, e, home(e) - g).wait_send())
-
-        @pl.when(has_next)
-        def _():
-            def one(i):
-                onward(PART, j, i).wait_send()
-                onward(LEVEL, j, i).wait_send()
-
-            loop(0, g, one)
-            onward(GRAM, j, 0).wait_send()
-            onward(CROSS, j, 0).wait_send()
+            back(1, j).wait_send()
+
+            @pl.when(reaches(1))
+            def _():
+                back(2, j).wait_send()
+
+        for d in range(1, REACH + 1):
+
+            @pl.when(reaches(d))
+            def _(d=d):
+                onward(PART, d, j).wait_send()
+                onward(LEVEL, d, j).wait_send()
+
+        for a in (GRAM, CROSS):
+            later_planes(lambda p: state(a, j, plane, p, p).wait_send())
 
     loop(0, per_device, finish)
+    later_planes(lambda p: state(DECAY, 0, plane, p, p).wait_send())
     for a in (RATES, MK, MQ):
-        others(lambda e: remote(a, 0, place, e, home(e)).wait_send())
-
-
-def group_body(
+        others(lambda e: remote(a, 0, place, e, e).wait_send())
+
+
+def plane_body(
     attn_query, attn_key, attn_value, mesa_query, mesa_key, log_decay, input_gate, regularizer
 ):
     rows = attn_query.shape[0]
     heads, size = regularizer.shape
     devices = lax.axis_size("seq")
-    g = WINDOW // rows
-    per_device, tokens = heads // g, WINDOW
+    g = WINDOW // (REACH * rows)
+    per_device, tokens, planes = heads // g, g * rows, devices // g
     per, chunks = rows // CHUNK, tokens // CHUNK
     cum = jnp.cumsum(log_decay.reshape(per, CHUNK, heads), axis=1)
     rates = jnp.concatenate([cum, input_gate.reshape(per, CHUNK, heads)], axis=0)
@@ -679,23 +770,31 @@
     anywhere = pl.BlockSpec(memory_space=pl.ANY)
     tall = pltpu.VMEM((tokens, per_device * size), BF16)
     levels = pltpu.VMEM((per_device, g, 8, rows), F32)
-    state = pltpu.VMEM((per_device, size, size), BF16)
+    total = pltpu.VMEM((per_device, size, size), BF16)
+    totals = pltpu.VMEM((per_device, planes, size, size), BF16)
     states = pltpu.VMEM((per_device, chunks, size, size), BF16)
+    slots = max(g, planes)
     return pl.pallas_call(
-        functools.partial(group_kernel, devices, g),
+        functools.partial(plane_kernel, devices, g),
         out_shape=(slab, slab),
         in_specs=[anywhere] * 5 + [vmem] * 2,
         out_specs=(anywhere, anywhere),
-        scratch_shapes=[tall] * 6
+        scratch_shapes=[tall] * 5
         + [pltpu.VMEM((per_device, g, 4 * per, CHUNK), F32)]
-        + [tall] * 4
-        + [levels] * 2
-        + [state] * 4
+        + [tall] * (2 + REACH + 2 * REACH)
+        + [levels] * (2 * REACH)
+        + [total] * 2
+        + [totals] * 2
+        + [
+            pltpu.VMEM((8, size), F32),
+            pltpu.VMEM((planes, 8, size), F32),
+            pltpu.VMEM((2, per_device, chunks, size, size), F32),
+        ]
         + [states] * 2
         + [
             pltpu.VMEM((tokens, per_device * size), F32),
-            pltpu.SemaphoreType.DMA((KINDS, per_device, g)),
-            pltpu.SemaphoreType.DMA((KINDS, per_device, g)),
+            pltpu.SemaphoreType.DMA((KINDS, per_device, slots)),
+            pltpu.SemaphoreType.DMA((KINDS, per_device, slots)),
             pltpu.SemaphoreType.DMA((KINDS, per_device)),
         ],
         compiler_params=pltpu.CompilerParams(
@@ -704,17 +803,18 @@
     )(attn_query, attn_key, attn_value, mesa_key, mesa_query, rates, regularizer)
 
 
-def fits_groups(mesh, rows, heads, size):
-    g = WINDOW // rows
+def fits_planes(mesh, rows, heads, size):
+    if WINDOW % (REACH * rows):
+        return False
+    g = WINDOW // (REACH * rows)
     return (
         size == CHUNK
-        and WINDOW % rows == 0
-        and g % 2 == 0
         and mesh.shape["seq"] % g == 0
         and heads % g == 0
+        and 2 <= heads // g <= 8
         and rows % CHUNK == 0
         and WAYS % (rows // CHUNK) == 0
-        and WINDOW % (CHUNK * WAYS) == 0
+        and g * rows % (CHUNK * WAYS) == 0
     )
 
 
@@ -723,8 +823,8 @@
 
     def body(*args):
         heads, size = args[7].shape
-        fits = fits_groups(mesh, args[0].shape[0], heads, size)
-        return (group_body if fits else slab_body)(*args)
+        fits = fits_planes(mesh, args[0].shape[0], heads, size)
+        return (plane_body if fits else slab_body)(*args)
 
     return jax.shard_map(
         body,

time: 171 us -> 158 us (0.924)
  Pallas kernels: 165 us -> 152 us
    pallas_call x1, Pallas kernels: 165 us -> 152 us  [plane_body(): pl.pallas_call(functools.partial(plane_kernel, devices, g), out_shape=(sl...]
where the time goes in v2:
time: 158 us
  Pallas kernels  152 us (96%)
  local copies, waits for them, and re-layouts  4.91 us (3%)
    pallas_call x1, Pallas kernels, plane_body(): pl.pallas_call(functools.partial(plane_kernel, devices, g), out_shape=(sl...  152 us
    unnamed x6, local copies, waits for them, and re-layouts  3.37 us

profile of v2, /device:TPU:29, one launch (start us, length us, event | category | flops | bytes accessed | tf_op | source)
XLA Modules:
  0.0 157.8 jit_solution(9268131382552628684)
XLA Ops:
  0.6 0.0 copy-start.1
  0.6 0.7 reshape.11
  1.4 0.0 copy-done.1
  1.4 0.1 copy.12
  1.5 0.2 reduce_window_sum.11
  1.7 0.1 copy.11
  1.8 0.6 pad.4.refs_5_
  2.4 151.9 %shard_map.95 = (bf16[256,2048]{1,0:T(8,128)(2,1)}, bf16[256,2048]{1,0:T(8,128)(2,1)}) custom-call(bf16[256,2048]{1,0:T(8,128)(2,1)} %refs_0_.1, bf16[256,2048]{1,0:T(8,128)(2,1)} %refs_1_.1, bf16[256,2048]{1,0:T(8,128)(2,1)} %refs_2_.1, bf16[256,2048]{1,0:T(8,128)(2,1)} %refs_3_.1, bf16[256,2048]{1,0:T(8,128)(2,1)} %refs_4_.1, f32[16,8,128]{2,1,0:T(8,128)} %pad.4.refs_5_, ...), custom_call_target="tpu_custom_call" | custom-call | tf_op jit(solution)/shard_map/pallas_call | solution.py:777
  154.4 0.0 copy-start
  154.4 2.4 %copy.15 = bf16[256,2048]{1,0:T(8,128)(2,1)} copy(bf16[256,2048]{1,0:T(8,128)(2,1)} %get-tuple-element.4) | data formatting | bytes 2097152
  156.8 0.0 copy-done
  156.8 1.0 copy.16
  (1 shorter events, 0.0 us)
Async XLA Ops:
  0.6 0.7 copy-start.1
  154.4 2.4 %copy-start = (bf16[256,2048]{1,0:T(8,128)(2,1)S(1)}, bf16[256,2048]{1,0:T(8,128)(2,1)}, u32[]{:S(2)}) copy-start(bf16[256,2048]{1,0:T(8,128)(2,1)} %get-tuple-element.5) | copy-start | bytes 3145732

commit v3 on v2

--- a/solution.py
+++ b/solution.py
@@ -209,12 +209,6 @@
     return lax.dot_general(a, b, dims, preferred_element_type=F32)
 
 
-def two_terms(a):
-    high = a.astype(BF16)
-    low = (a - high.astype(F32)).astype(BF16)
-    return jnp.concatenate([high, low], axis=1)
-
-
 def score_blocks(queries, k_ref, base, count, rows, masks):
     scores, top = [], None
     for j in range(count):
@@ -274,30 +268,34 @@
     l_ref[i] = jnp.transpose(level)[:8, :]
 
 
-def attend_far(q_ref, k_ref, v_ref, o_ref, l_ref, rows):
+def attend_far(q_ref, k_ref, v_ref, o_ref, l_ref, rows, done):
     blocks = k_ref.shape[0] // rows
     beyond = index_gap(rows) < 0
     for i in range(blocks):
         masks = [beyond] + [None] * (blocks - i - 1)
         store_part(partial(q_ref, k_ref, v_ref, i, i * rows, masks, rows), o_ref, l_ref, i, rows)
-
-
-def attend_middle(q_ref, k_ref, v_ref, o_in, l_in, o_ref, l_ref, rows):
+        done(i)
+
+
+def attend_middle(q_ref, k_ref, v_ref, o_in, l_in, o_ref, l_ref, rows, ready, done):
     blocks = k_ref.shape[0] // rows
 
     def one(i, carry):
         part = partial(q_ref, k_ref, v_ref, i, 0, [None] * blocks, rows)
+        ready(i)
         store_part(joined(part, o_in, l_in, i, rows), o_ref, l_ref, i, rows)
+        done(i)
         return carry
 
     lax.fori_loop(0, blocks, one, 0)
 
 
-def attend_own(q_ref, k_ref, v_ref, o_in, l_in, out_ref, rows, done):
+def attend_own(q_ref, k_ref, v_ref, o_in, l_in, out_ref, rows, ready, done):
     blocks = k_ref.shape[0] // rows
     causal = index_gap(rows) >= 0
     for i in range(blocks):
         part = partial(q_ref, k_ref, v_ref, i, 0, [None] * i + [causal], rows)
+        ready(i)
         level, total, summed = joined(part, o_in, l_in, i, rows)
         out_ref[block_of(i, rows), :] = (summed / total).astype(BF16)
         done(i)
@@ -384,60 +382,64 @@
 
 
 def solve_all(q_ref, k_ref, rates_ref, ridge_ref, gram_ref, x_ref):
-    ridge = ridge_ref
     per = rates_ref.shape[1] // 4
     chunks = rates_ref.shape[0] * per
+    ways = math.gcd(chunks, 8)
+    ridge = column_form(ridge_ref)
+    later = lax.broadcasted_iota(jnp.int32, (CHUNK, CHUNK), 1) >= lax.broadcasted_iota(
+        jnp.int32, (CHUNK, CHUNK), 0
+    )
 
     def group(g, carry):
-        ids = chunk_ids(g, per)
-        mixes = [mix_of(rates_ref, c) for c in ids]
-        keys = [k_ref[span(c, per), :] for c in ids]
-        grams = [gram_ref[flat(c, per)] for c in ids]
-        sides = [
-            jnp.concatenate(
-                [jnp.concatenate([a, a], axis=1), jnp.concatenate([k, k], axis=1)], axis=0
+        ids = chunk_ids(g, per, ways)
+        mixes, starts, keys, sides, state = [], [], [], [], []
+        for c in ids:
+            cum, gate = rates_of(rates_ref, c)
+            gap = jnp.where(later, cum - column_form(cum), masked_score)
+            mixes.append(jnp.exp(gap) * column_form(gate))
+            starts.append(jnp.exp(cum))
+            keys.append(k_ref[span(c, per), :])
+            sides.append(
+                jnp.concatenate([gram_ref[flat(c, per)], jnp.transpose(keys[-1])], axis=1)
             )
-            for a, k in zip(grams, keys)
-        ]
-        stacks = [jnp.concatenate([k, k], axis=0) for k in keys]
-        state = []
-        for c in ids:
-            q = q_ref[span(c, per), :].astype(F32)
-            state.append((jnp.zeros_like(q), q, q, jnp.sum(q * q, axis=1, keepdims=True)))
-
-        def sweep(n, state):
-            both = [dot(two_terms(s[2]), side, NT) for s, side in zip(state, sides)]
-            local = [
-                dot(two_terms(m[0] * b[:, CHUNK:]), k) for m, b, k in zip(mixes, both, stacks)
+            q = jnp.transpose(q_ref[span(c, per), :]).astype(F32)
+            state.append((jnp.zeros_like(q), q, q, jnp.sum(q * q, axis=0, keepdims=True)))
+        for sweep_index in range(CG_ITERS):
+            directions = [s[2].astype(BF16) for s in state]
+            products = [dot(k, p) for k, p in zip(keys, directions)]
+            images = [
+                dot(
+                    side,
+                    jnp.concatenate(
+                        [(start * p.astype(F32)).astype(BF16), (mix * b).astype(BF16)], axis=0
+                    ),
+                )
+                for side, start, mix, p, b in zip(sides, starts, mixes, directions, products)
             ]
-            out = []
-            for (x, r, p, rr), b, l, m in zip(state, both, local, mixes):
-                a = m[1] * b[:, :CHUNK] + l + ridge * p
-                alpha = rr / (jnp.sum(p * a, axis=1, keepdims=True) + 1e-6)
+            for w, a in enumerate(images):
+                x, r, _, rr = state[w]
+                p = directions[w].astype(F32)
+                a = a + ridge * p
+                alpha = rr / (jnp.sum(p * a, axis=0, keepdims=True) + 1e-6)
                 x = x + alpha * p
                 r = r - alpha * a
-                new = jnp.sum(r * r, axis=1, keepdims=True)
-                p = r + (new / (rr + 1e-6)) * p
-                out.append((x, r, p, new))
-            return tuple(out)
-
-        state = lax.fori_loop(0, CG_ITERS, sweep, tuple(state))
+                new = jnp.sum(r * r, axis=0, keepdims=True)
+                state[w] = (x, r, r + (new / (rr + 1e-6)) * p, new)
         for c, s in zip(ids, state):
-            x_ref[span(c, per), :] = s[0]
+            x_ref[span(c, per), :] = jnp.transpose(s[0].astype(BF16))
         return carry
 
-    lax.fori_loop(0, chunks // WAYS, group, 0)
+    lax.fori_loop(0, chunks // ways, group, 0)
 
 
 def read_out(k_ref, v_ref, rates_ref, cross_ref, x_ref, out_ref, slab):
     per = rates_ref.shape[1] // 4
     for c in chunk_ids(slab, per, per):
         mix, start = mix_of(rates_ref, c)
-        keys, values, cross = k_ref[span(c, per), :], v_ref[span(c, per), :], cross_ref[flat(c, per)]
-        x = two_terms(x_ref[span(c, per), :])
-        products = dot(x, jnp.concatenate([keys, keys], axis=1), NT)
-        rows = start * dot(x, jnp.concatenate([cross, cross], axis=0))
-        rows = rows + dot(two_terms(mix * products), jnp.concatenate([values, values], axis=0))
+        x = x_ref[span(c, per), :]
+        products = dot(x, k_ref[span(c, per), :], NT)
+        rows = start * dot(x, cross_ref[flat(c, per)])
+        rows = rows + dot((mix * products).astype(BF16), v_ref[span(c, per), :])
         out_ref[span(c, per), :] = rows.astype(BF16)
 
 
@@ -445,6 +447,17 @@
 Q, K, V, MK, MQ, RATES, ATT, OUT, GRAM, CROSS, DECAY = range(11)
 QX, PART, LEVEL = (11, 13, 15)
 KINDS = 17
+
+
+def push_order(heads):
+    order = [(Q, 0), (K, 0), (V, 0), (Q, 1)]
+    order += [(Q, j) for j in range(2, min(3, heads))]
+    order += [(MK, j) for j in range(heads)]
+    order += [(Q, j) for j in range(3, heads)]
+    order += [(K, 1), (V, 1), (MQ, 0), (MQ, 1)]
+    for j in range(2, heads):
+        order += [(K, j), (V, j), (MQ, j)]
+    return order
 
 
 def plane_kernel(n, g, *refs):
@@ -462,13 +475,9 @@
     att, out = homes
     rows, size = ins[0].shape[0], ridge_in.shape[1]
     per_device = rates.shape[0]
-    wide = per_device * size
     planes = n // g
     group, me = lax.axis_index("groups"), lax.axis_index("seq")
     plane, place = me // g, lax.rem(me, g)
-
-    def row_block(ref, s):
-        return ref.at[pl.ds(pl.multiple_of(s * rows, rows), rows), :]
 
     def head_col(ref, j):
         return ref.at[:, pl.ds(pl.multiple_of(j * size, size), size)]
@@ -480,10 +489,7 @@
         ]
 
     def ends(a, j, source, target):
-        if a in (MK, MQ):
-            src = ins[a].at[:, pl.ds(pl.multiple_of(target * wide, wide), wide)]
-            return src, row_block(bufs[a], source)
-        if a in (Q, K, V):
+        if a in (Q, K, V, MK, MQ):
             return head_col(ins[a], target * per_device + j), cell(bufs[a], source, j)
         if a == RATES:
             return rates_in.at[pl.ds(target * per_device, per_device)], rates.at[:, source]
@@ -510,17 +516,27 @@
         src, dst = ends(a, j, place, place)
         return pltpu.make_async_copy(src, dst, own.at[a, j])
 
-    def back(d, j):
+    def back(d, j, e):
         return copy_to(
-            head_col(later[d - 1], j), head_col(later[d], j), QX + d - 1, j, 0, 0, me - g
+            cell(later[d - 1], e, j), cell(later[d], e, j), QX + d - 1, j, e, e, me - g
         )
 
-    def onward(a, d, j):
+    def onward(a, d, j, i):
         if a == PART:
-            src, dst = head_col(o_out[d], j), head_col(o_in[d], j)
+            src, dst = cell(o_out[d], i, j), cell(o_in[d], i, j)
         else:
-            src, dst = l_out[d].at[j], l_in[d].at[j]
-        return copy_to(src, dst, a + d - 1, j, 0, 0, me + g)
+            src, dst = l_out[d].at[j, i], l_in[d].at[j, i]
+        return copy_to(src, dst, a + d - 1, j, i, i, me + g)
+
+    def pass_on(d, j, i):
+        onward(PART, d, j, i).start()
+        onward(LEVEL, d, j, i).start()
+
+    def take(d, j, i):
+        @pl.when(has_previous)
+        def _():
+            onward(PART, d, j, i).wait_recv()
+            onward(LEVEL, d, j, i).wait_recv()
 
     def state(a, j, source, target, peer_plane):
         if a == DECAY:
@@ -575,8 +591,8 @@
     pl.semaphore_wait(barrier, g - 1 + planes - 1)
 
     push(RATES, 0)
-    for j in range(per_device):
-        push(Q, j)
+    for a, j in push_order(per_device):
+        push(a, j)
 
     @pl.when(jnp.logical_not(has_previous))
     def _():
@@ -584,37 +600,41 @@
             o_in[d][...] = jnp.zeros_like(o_in[d])
             l_in[d][...] = jnp.full_like(l_in[d], masked_score)
 
+    def near_first(act):
+        loop(0, g, lambda t: act(place ^ t))
+
     def forward(j):
-        arrive(Q, j)
-
-        @pl.when(has_previous)
-        def _():
-            back(1, j).start()
+        def one(e):
+            @pl.when(e == place)
+            def _():
+                local(Q, j).wait()
+
+            @pl.when(e != place)
+            def _():
+                remote(Q, j, e, place, e).wait_recv()
+
+            @pl.when(has_previous)
+            def _():
+                back(1, j, e).start()
+
+        near_first(one)
 
     def relay(j):
         @pl.when(reaches(1))
         def _():
-            back(1, j).wait_recv()
-
-            @pl.when(has_previous)
-            def _():
-                back(2, j).start()
-
-    def push_values(j):
-        push(K, j)
-        push(V, j)
-
-    for j in range(per_device):
-        forward(j)
-        if j == 0:
-            push(MK, 0)
-            push_values(0)
-        if j > 0:
-            relay(j - 1)
-    push(MQ, 0)
-    push_values(1)
+            def one(e):
+                back(1, j, e).wait_recv()
+
+                @pl.when(has_previous)
+                def _():
+                    back(2, j, e).start()
+
+            near_first(one)
+
+    forward(0)
+    forward(1)
+    relay(0)
     arrive(RATES, 0)
-    arrive(MK, 0)
 
     def head_totals(a, j, others_ref):
         decay = state_totals(
@@ -632,15 +652,20 @@
         )
 
     def gram_head(j):
+        arrive(MK, j)
         decay = head_totals(GRAM, j, mk)
         decay_out[pl.ds(j, 1), :] = jnp.broadcast_to(decay, (1, size))
 
-    loop(0, per_device, gram_head)
-    later_planes(lambda p: state(DECAY, 0, plane, p, p).start())
-    relay(per_device - 1)
-
     def step(s):
         far, middle, near, last = s, s - 1, s - 2, s - 3
+
+        @pl.when(far + 1 < per_device)
+        def _():
+            relay(far + 1)
+
+        @pl.when(far + 2 < per_device)
+        def _():
+            forward(far + 2)
 
         @pl.when(far < per_device)
         def _():
@@ -648,19 +673,13 @@
             arrive(K, j)
             arrive(V, j)
 
-            @pl.when(j + 2 < per_device)
-            def _():
-                push_values(j + 2)
-
             @pl.when(reaches(2))
             def _():
-                back(2, j).wait_recv()
+                loop(0, g, lambda e: back(2, j, e).wait_recv())
                 attend_far(
                     head_col(later[2], j), head_col(k, j), head_col(v, j),
-                    head_col(o_out[2], j), l_out[2].at[j], rows,
+                    head_col(o_out[2], j), l_out[2].at[j], rows, lambda i: pass_on(2, j, i),
                 )
-                onward(PART, 2, j).start()
-                onward(LEVEL, 2, j).start()
 
         @pl.when((middle >= 0) & (middle < per_device))
         def _():
@@ -668,25 +687,19 @@
 
             @pl.when(reaches(1))
             def _():
-                @pl.when(has_previous)
-                def _():
-                    onward(PART, 2, j).wait_recv()
-                    onward(LEVEL, 2, j).wait_recv()
-
                 attend_middle(
                     head_col(later[1], j), head_col(k, j), head_col(v, j),
                     head_col(o_in[2], j), l_in[2].at[j],
                     head_col(o_out[1], j), l_out[1].at[j], rows,
+                    lambda i: take(2, j, i), lambda i: pass_on(1, j, i),
                 )
-                onward(PART, 1, j).start()
-                onward(LEVEL, 1, j).start()
 
             @pl.when(j == 0)
             def _():
-                arrive(MQ, 0)
                 loop(0, plane, lambda p: state(DECAY, 0, p, plane, p).wait_recv())
 
             head_starts(GRAM, j, gram)
+            arrive(MQ, j)
             solve_all(
                 head_col(mq, j), head_col(mk, j), rates.at[j],
                 ridge_in[pl.ds(place * per_device + j, 1), :], gram.at[j], head_col(x, j),
@@ -695,17 +708,17 @@
         @pl.when((near >= 0) & (near < per_device))
         def _():
             j = near
-
-            @pl.when(has_previous)
-            def _():
-                onward(PART, 1, j).wait_recv()
-                onward(LEVEL, 1, j).wait_recv()
-
             attend_own(
                 head_col(q, j), head_col(k, j), head_col(v, j), head_col(o_in[1], j),
-                l_in[1].at[j], head_col(att, j), rows, lambda i: give(ATT, j, i),
+                l_in[1].at[j], head_col(att, j), rows,
+                lambda i: take(1, j, i), lambda i: give(ATT, j, i),
             )
             head_totals(CROSS, j, att)
+
+        @pl.when(s == 0)
+        def _():
+            loop(0, per_device, gram_head)
+            later_planes(lambda p: state(DECAY, 0, plane, p, p).start())
 
         @pl.when(last >= 0)
         def _():
@@ -726,31 +739,32 @@
     def finish(j):
         for a in (ATT, OUT):
             arrive(a, j)
-        for a in (Q, K, V, ATT, OUT):
+        for a in (Q, K, V, MK, MQ, ATT, OUT):
             others(lambda e: remote(a, j, place, e, e).wait_send())
 
-        @pl.when(has_previous)
-        def _():
-            back(1, j).wait_send()
-
-            @pl.when(reaches(1))
+        def block(i):
+            @pl.when(has_previous)
             def _():
-                back(2, j).wait_send()
-
-        for d in range(1, REACH + 1):
-
-            @pl.when(reaches(d))
-            def _(d=d):
-                onward(PART, d, j).wait_send()
-                onward(LEVEL, d, j).wait_send()
-
+                back(1, j, i).wait_send()
+
+                @pl.when(reaches(1))
+                def _():
+                    back(2, j, i).wait_send()
+
+            for d in range(1, REACH + 1):
+
+                @pl.when(reaches(d))
+                def _(d=d):
+                    onward(PART, d, j, i).wait_send()
+                    onward(LEVEL, d, j, i).wait_send()
+
+        loop(0, g, block)
         for a in (GRAM, CROSS):
             later_planes(lambda p: state(a, j, plane, p, p).wait_send())
 
     loop(0, per_device, finish)
     later_planes(lambda p: state(DECAY, 0, plane, p, p).wait_send())
-    for a in (RATES, MK, MQ):
-        others(lambda e: remote(a, 0, place, e, e).wait_send())
+    others(lambda e: remote(RATES, 0, place, e, e).wait_send())
 
 
 def plane_body(
@@ -792,7 +806,7 @@
         ]
         + [states] * 2
         + [
-            pltpu.VMEM((tokens, per_device * size), F32),
+            tall,
             pltpu.SemaphoreType.DMA((KINDS, per_device, slots)),
             pltpu.SemaphoreType.DMA((KINDS, per_device, slots)),
             pltpu.SemaphoreType.DMA((KINDS, per_device)),
@@ -809,6 +823,7 @@
     g = WINDOW // (REACH * rows)
     return (
         size == CHUNK
+        and g & (g - 1) == 0
         and mesh.shape["seq"] % g == 0
         and heads % g == 0
         and 2 <= heads // g <= 8

time: 158 us -> 120 us (0.76)
  Pallas kernels: 152 us -> 113 us
    pallas_call x1, Pallas kernels: 152 us -> 113 us  [plane_body(): pl.pallas_call(functools.partial(plane_kernel, devices, g), out_shape=(sl...]
where the time goes in v3:
time: 120 us; the launch traced here: 119 us
  Pallas kernels  113 us (94%)
  local copies, waits for them, and re-layouts  4.91 us (4%)
    pallas_call x1, Pallas kernels, plane_body(): pl.pallas_call(functools.partial(plane_kernel, devices, g), out_shape=(sl...  113 us
    unnamed x6, local copies, waits for them, and re-layouts  3.37 us

profile of v3, /device:TPU:29, one launch (start us, length us, event | category | flops | bytes accessed | tf_op | source)
XLA Modules:
  0.0 119.1 jit_solution(9254878604819476655)
XLA Ops:
  0.6 0.0 copy-start.1
  0.6 0.7 reshape.11
  1.4 0.0 copy-done.1
  1.4 0.1 copy.12
  1.5 0.2 reduce_window_sum.11
  1.7 0.1 copy.11
  1.8 0.6 pad.4.refs_5_
  2.4 113.3 %shard_map.95 = (bf16[256,2048]{1,0:T(8,128)(2,1)}, bf16[256,2048]{1,0:T(8,128)(2,1)}) custom-call(bf16[256,2048]{1,0:T(8,128)(2,1)} %refs_0_.1, bf16[256,2048]{1,0:T(8,128)(2,1)} %refs_1_.1, bf16[256,2048]{1,0:T(8,128)(2,1)} %refs_2_.1, bf16[256,2048]{1,0:T(8,128)(2,1)} %refs_3_.1, bf16[256,2048]{1,0:T(8,128)(2,1)} %refs_4_.1, f32[16,8,128]{2,1,0:T(8,128)} %pad.4.refs_5_, ...), custom_call_target="tpu_custom_call" | custom-call | tf_op jit(solution)/shard_map/pallas_call | solution.py:791
  115.7 0.0 copy-start
  115.7 2.4 %copy.15 = bf16[256,2048]{1,0:T(8,128)(2,1)} copy(bf16[256,2048]{1,0:T(8,128)(2,1)} %get-tuple-element.4) | data formatting | bytes 2097152
  118.1 0.0 copy-done
  118.1 1.0 copy.16
  (1 shorter events, 0.0 us)
Async XLA Ops:
  0.6 0.7 copy-start.1
  115.7 2.4 %copy-start = (bf16[256,2048]{1,0:T(8,128)(2,1)S(1)}, bf16[256,2048]{1,0:T(8,128)(2,1)}, u32[]{:S(2)}) copy-start(bf16[256,2048]{1,0:T(8,128)(2,1)} %get-tuple-element.5) | copy-start | bytes 3145732

commit v4 on v3

--- a/solution.py
+++ b/solution.py
@@ -252,9 +252,13 @@
     return top * scale, total, summed
 
 
+def columns(row, size):
+    return jnp.transpose(jnp.broadcast_to(row, (size, row.shape[1])))
+
+
 def joined(part, o_ref, l_ref, i, rows):
     level, total, summed = part
-    earlier = jnp.transpose(jnp.broadcast_to(l_ref[i][:1, :], (summed.shape[1], rows)))
+    earlier = columns(l_ref[i], summed.shape[1])
     peak = jnp.maximum(earlier, level)
     share_own, share_earlier = jnp.exp2(level - peak), jnp.exp2(earlier - peak)
     summed = summed * share_own + o_ref[block_of(i, rows), :].astype(F32) * share_earlier
@@ -263,42 +267,56 @@
 
 def store_part(part, o_ref, l_ref, i, rows):
     level, total, summed = part
-    o_ref[block_of(i, rows), :] = (summed / total).astype(BF16)
+    o_ref[block_of(i, rows), :] = (summed / total).astype(o_ref.dtype)
     level = jnp.broadcast_to(level + jnp.log2(total), summed.shape)
-    l_ref[i] = jnp.transpose(level)[:8, :]
+    l_ref[i] = jnp.transpose(level)[:1, :]
 
 
 def attend_far(q_ref, k_ref, v_ref, o_ref, l_ref, rows, done):
     blocks = k_ref.shape[0] // rows
     beyond = index_gap(rows) < 0
-    for i in range(blocks):
-        masks = [beyond] + [None] * (blocks - i - 1)
-        store_part(partial(q_ref, k_ref, v_ref, i, i * rows, masks, rows), o_ref, l_ref, i, rows)
+    for i in range(0, blocks, 2):
+        for n in (i, i + 1):
+            masks = [beyond] + [None] * (blocks - n - 1)
+            part = partial(q_ref, k_ref, v_ref, n, n * rows, masks, rows)
+            store_part(part, o_ref, l_ref, n, rows)
         done(i)
+        done(i + 1)
 
 
 def attend_middle(q_ref, k_ref, v_ref, o_in, l_in, o_ref, l_ref, rows, ready, done):
     blocks = k_ref.shape[0] // rows
 
-    def one(i, carry):
-        part = partial(q_ref, k_ref, v_ref, i, 0, [None] * blocks, rows)
-        ready(i)
-        store_part(joined(part, o_in, l_in, i, rows), o_ref, l_ref, i, rows)
-        done(i)
+    def two(t, carry):
+        pair = (2 * t, 2 * t + 1)
+        ready(t)
+        for i in pair:
+            part = partial(q_ref, k_ref, v_ref, i, 0, [None] * blocks, rows)
+            store_part(joined(part, o_in, l_in, i, rows), o_ref, l_ref, i, rows)
+        for i in pair:
+            done(i)
         return carry
 
-    lax.fori_loop(0, blocks, one, 0)
-
-
-def attend_own(q_ref, k_ref, v_ref, o_in, l_in, out_ref, rows, ready, done):
-    blocks = k_ref.shape[0] // rows
+    lax.fori_loop(0, blocks // 2, two, 0)
+
+
+def attend_own(q_ref, k_ref, v_ref, o_ref, l_ref, rows):
     causal = index_gap(rows) >= 0
-    for i in range(blocks):
+    for i in range(k_ref.shape[0] // rows):
         part = partial(q_ref, k_ref, v_ref, i, 0, [None] * i + [causal], rows)
-        ready(i)
-        level, total, summed = joined(part, o_in, l_in, i, rows)
-        out_ref[block_of(i, rows), :] = (summed / total).astype(BF16)
-        done(i)
+        store_part(part, o_ref, l_ref, i, rows)
+
+
+def attend_last(o_own, l_own, o_in, l_in, out_ref, rows, ready, done):
+    blocks = o_own.shape[0] // rows
+    for i in range(0, blocks, 2):
+        ready(i // 2)
+        for n in (i, i + 1):
+            own = (columns(l_own[n], o_own.shape[1]), 1.0, o_own[block_of(n, rows), :])
+            level, total, summed = joined(own, o_in, l_in, n, rows)
+            out_ref[block_of(n, rows), :] = (summed / total).astype(BF16)
+        for n in (i, i + 1):
+            done(n)
 
 
 def flat(c, per):
@@ -342,7 +360,7 @@
     return mix, jnp.exp(col)
 
 
-def state_totals(k_ref, other_ref, rates_ref, zero_ref, total_ref):
+def state_totals(k_ref, other_ref, rates_ref, zero_ref):
     per = rates_ref.shape[1] // 4
     chunks = rates_ref.shape[0] * per
 
@@ -358,18 +376,13 @@
     state, decay = lax.fori_loop(
         0, chunks // WAYS, step, (jnp.zeros((CHUNK, CHUNK), F32), jnp.ones((1, 1), F32))
     )
-    total_ref[...] = state.astype(BF16)
+    zero_ref[chunks] = state
     return decay
 
 
-def state_starts(rates_ref, zero_ref, totals_ref, decay_ref, count, starts_ref):
+def state_starts(rates_ref, zero_ref, first_ref, starts_ref):
     per = rates_ref.shape[1] // 4
     chunks = rates_ref.shape[0] * per
-
-    def plane(p, first):
-        return decay_ref(p) * first + totals_ref[p].astype(F32)
-
-    first = lax.fori_loop(0, count, plane, jnp.zeros((CHUNK, CHUNK), F32))
 
     def step(g, first):
         for c in chunk_ids(g, per):
@@ -378,7 +391,7 @@
             first = first * jnp.exp(cum[:, CHUNK - 1 :])
         return first
 
-    lax.fori_loop(0, chunks // WAYS, step, first)
+    lax.fori_loop(0, chunks // WAYS, step, first_ref[...].astype(F32))
 
 
 def solve_all(q_ref, k_ref, rates_ref, ridge_ref, gram_ref, x_ref):
@@ -444,19 +457,19 @@
 
 
 REACH = 2
-Q, K, V, MK, MQ, RATES, ATT, OUT, GRAM, CROSS, DECAY = range(11)
-QX, PART, LEVEL = (11, 13, 15)
-KINDS = 17
+Q, K, V, MK, MQ, RATES, ATT, OUT, GRAM, CROSS = range(10)
+QX, PART, LEVEL = (10, 12, 14)
+KINDS = 16
+BY_HEAD = (K, V, MK, MQ, GRAM, CROSS, QX + 1)
 
 
 def push_order(heads):
-    order = [(Q, 0), (K, 0), (V, 0), (Q, 1)]
-    order += [(Q, j) for j in range(2, min(3, heads))]
-    order += [(MK, j) for j in range(heads)]
-    order += [(Q, j) for j in range(3, heads)]
-    order += [(K, 1), (V, 1), (MQ, 0), (MQ, 1)]
-    for j in range(2, heads):
-        order += [(K, j), (V, j), (MQ, j)]
+    order = [(MK, 0), (Q, 0), (MQ, 0), (Q, 1), (K, 0), (V, 0)]
+    for j in range(1, heads):
+        order += [(MK, j), (MQ, j)]
+        order += [(Q, 2)] if j == 1 and heads > 2 else []
+        order += [(K, j), (V, j)]
+        order += [(Q, j + 2)] if j + 2 < heads else []
     return order
 
 
@@ -467,10 +480,11 @@
     later = (refs[9],) + refs[17:19]
     o_out, o_in = (None,) + refs[19:21], (None,) + refs[21:23]
     l_out, l_in = (None,) + refs[23:25], (None,) + refs[25:27]
-    total_out, total_in = {GRAM: refs[27], CROSS: refs[28]}, {GRAM: refs[29], CROSS: refs[30]}
-    decay_out, decay_in, zero = refs[31:34]
-    gram, cross, x = refs[34:37]
-    send, recv, own = refs[37:40]
+    first_out, first_in = {GRAM: refs[27], CROSS: refs[28]}, {GRAM: refs[29], CROSS: refs[30]}
+    decays, zero = refs[31:33]
+    gram, cross, x = refs[33:36]
+    o_own, l_own = refs[36:38]
+    send, by_block, by_head, by_pair, at_end, own, own_end = refs[38:45]
     q, k, v, mk, mq = bufs
     att, out = homes
     rows, size = ins[0].shape[0], ridge_in.shape[1]
@@ -495,30 +509,43 @@
             return rates_in.at[pl.ds(target * per_device, per_device)], rates.at[:, source]
         return cell(homes[a - ATT], target, j), head_col(results[a - ATT], source * per_device + j)
 
-    def copy_to(src, dst, a, j, sent, got, peer):
+    def arrival(a, j, i):
+        if a in (Q, QX):
+            return by_block.at[(Q, QX).index(a), j, i]
+        if a in BY_HEAD:
+            return by_head.at[BY_HEAD.index(a), j]
+        if a >= PART:
+            return by_pair.at[a - PART, j, i // 2]
+        return at_end.at[a - RATES]
+
+    def copy_to(src, dst, a, j, i, peer):
         return pltpu.make_async_remote_copy(
             src_ref=src,
             dst_ref=dst,
-            send_sem=send.at[a, j, sent],
-            recv_sem=recv.at[a, j, got],
+            send_sem=send.at[a],
+            recv_sem=arrival(a, j, i),
             device_id=(group, peer),
             device_id_type=pl.DeviceIdType.MESH,
         )
 
+    def bytes_of(ref, a, j=0, i=0):
+        return copy_to(ref, ref, a, j, i, me)
+
     def home(e):
         return plane * g + e
 
     def remote(a, j, source, target, peer):
         src, dst = ends(a, j, source, target)
-        return copy_to(src, dst, a, j, target, source, home(peer))
+        return copy_to(src, dst, a, j, source, home(peer))
 
     def local(a, j):
         src, dst = ends(a, j, place, place)
-        return pltpu.make_async_copy(src, dst, own.at[a, j])
+        sem = own_end.at[a - RATES] if a in (RATES, ATT, OUT) else own.at[a, j]
+        return pltpu.make_async_copy(src, dst, sem)
 
     def back(d, j, e):
         return copy_to(
-            cell(later[d - 1], e, j), cell(later[d], e, j), QX + d - 1, j, e, e, me - g
+            cell(later[d - 1], e, j), cell(later[d], e, j), QX + d - 1, j, e, me - g
         )
 
     def onward(a, d, j, i):
@@ -526,24 +553,22 @@
             src, dst = cell(o_out[d], i, j), cell(o_in[d], i, j)
         else:
             src, dst = l_out[d].at[j, i], l_in[d].at[j, i]
-        return copy_to(src, dst, a + d - 1, j, i, i, me + g)
+        return copy_to(src, dst, a + d - 1, j, i, me + g)
 
     def pass_on(d, j, i):
         onward(PART, d, j, i).start()
         onward(LEVEL, d, j, i).start()
 
-    def take(d, j, i):
+    def take(d, j, t):
         @pl.when(has_previous)
         def _():
-            onward(PART, d, j, i).wait_recv()
-            onward(LEVEL, d, j, i).wait_recv()
-
-    def state(a, j, source, target, peer_plane):
-        if a == DECAY:
-            src, dst = decay_out, decay_in.at[source]
-        else:
-            src, dst = total_out[a].at[j], total_in[a].at[j, source]
-        return copy_to(src, dst, a, j, target, source, peer_plane * g + place)
+            both = pl.ds(pl.multiple_of(2 * t * rows, rows), 2 * rows)
+            sums = head_col(o_in[d], j).at[both, :]
+            bytes_of(sums, PART + d - 1, j, 2 * t).wait_recv()
+            bytes_of(l_in[d].at[j, pl.ds(2 * t, 2)], LEVEL + d - 1, j, 2 * t).wait_recv()
+
+    def state(a, j):
+        return copy_to(first_out[a].at[j], first_in[a].at[j], a, j, 0, me + g)
 
     def loop(first, last, act):
         def one(t, carry):
@@ -555,9 +580,6 @@
     def others(act):
         loop(1, g, lambda t: act(lax.rem(place + t, g)))
 
-    def later_planes(act):
-        loop(plane + 1, planes, act)
-
     def signal(peer):
         pl.semaphore_signal(
             barrier, inc=1, device_id=(group, peer), device_id_type=pl.DeviceIdType.MESH
@@ -568,7 +590,10 @@
         local(a, j).start()
 
     def arrive(a, j):
-        others(lambda e: remote(a, j, e, place, e).wait_recv())
+        if a == RATES:
+            bytes_of(rates.at[:, : g - 1], a).wait_recv()
+        else:
+            bytes_of(head_col(bufs[a], j).at[: (g - 1) * rows, :], a, j).wait_recv()
         local(a, j).wait()
 
     def give(a, j, e):
@@ -587,8 +612,17 @@
 
     barrier = pltpu.get_barrier_semaphore()
     others(lambda e: signal(home(e)))
-    loop(1, planes, lambda t: signal(lax.rem(plane + t, planes) * g + place))
-    pl.semaphore_wait(barrier, g - 1 + planes - 1)
+
+    @pl.when(has_previous)
+    def _():
+        signal(me - g)
+
+    @pl.when(reaches(1))
+    def _():
+        signal(me + g)
+
+    neighbours = has_previous.astype(jnp.int32) + reaches(1).astype(jnp.int32)
+    pl.semaphore_wait(barrier, g - 1 + neighbours)
 
     push(RATES, 0)
     for a, j in push_order(per_device):
@@ -599,6 +633,8 @@
         for d in range(1, REACH + 1):
             o_in[d][...] = jnp.zeros_like(o_in[d])
             l_in[d][...] = jnp.full_like(l_in[d], masked_score)
+        for a in (GRAM, CROSS):
+            first_in[a][...] = jnp.zeros_like(first_in[a])
 
     def near_first(act):
         loop(0, g, lambda t: act(place ^ t))
@@ -631,72 +667,52 @@
 
             near_first(one)
 
-    forward(0)
-    forward(1)
-    relay(0)
     arrive(RATES, 0)
 
     def head_totals(a, j, others_ref):
-        decay = state_totals(
-            head_col(mk, j), head_col(others_ref, j), rates.at[j], zero.at[a - GRAM, j],
-            total_out[a].at[j],
+        return state_totals(
+            head_col(mk, j), head_col(others_ref, j), rates.at[j], zero.at[a - GRAM, j]
         )
-        later_planes(lambda p: state(a, j, plane, p, p).start())
-        return decay
+
+    def hand_on(a, j):
+        @pl.when(has_previous)
+        def _():
+            state(a, j).wait_recv()
+
+        @pl.when(reaches(1))
+        def _():
+            first = first_in[a][j].astype(F32)
+            following = decays[pl.ds(j, 1), :] * first + zero[a - GRAM, j, zero.shape[2] - 1]
+            first_out[a][j] = following.astype(BF16)
+            state(a, j).start()
 
     def head_starts(a, j, starts_ref):
-        loop(0, plane, lambda p: state(a, j, p, plane, p).wait_recv())
-        state_starts(
-            rates.at[j], zero.at[a - GRAM, j], total_in[a].at[j],
-            lambda p: decay_in[p, pl.ds(j, 1), :], plane, starts_ref.at[j],
-        )
-
-    def gram_head(j):
+        state_starts(rates.at[j], zero.at[a - GRAM, j], first_in[a].at[j], starts_ref.at[j])
+
+    def total_head(j):
         arrive(MK, j)
         decay = head_totals(GRAM, j, mk)
-        decay_out[pl.ds(j, 1), :] = jnp.broadcast_to(decay, (1, size))
+        decays[pl.ds(j, 1), :] = jnp.broadcast_to(decay, (1, size))
+
+        @pl.when(jnp.logical_not(has_previous))
+        def _():
+            hand_on(GRAM, j)
 
     def step(s):
-        far, middle, near, last = s, s - 1, s - 2, s - 3
-
-        @pl.when(far + 1 < per_device)
-        def _():
-            relay(far + 1)
-
-        @pl.when(far + 2 < per_device)
-        def _():
-            forward(far + 2)
-
-        @pl.when(far < per_device)
-        def _():
-            j = far
-            arrive(K, j)
-            arrive(V, j)
-
-            @pl.when(reaches(2))
+        first, middle, near, last = s, s - 1, s - 2, s - 3
+
+        @pl.when(s == 0)
+        def _():
+            total_head(0)
+            forward(0)
+
+        @pl.when(first < per_device)
+        def _():
+            j = first
+
+            @pl.when(has_previous)
             def _():
-                loop(0, g, lambda e: back(2, j, e).wait_recv())
-                attend_far(
-                    head_col(later[2], j), head_col(k, j), head_col(v, j),
-                    head_col(o_out[2], j), l_out[2].at[j], rows, lambda i: pass_on(2, j, i),
-                )
-
-        @pl.when((middle >= 0) & (middle < per_device))
-        def _():
-            j = middle
-
-            @pl.when(reaches(1))
-            def _():
-                attend_middle(
-                    head_col(later[1], j), head_col(k, j), head_col(v, j),
-                    head_col(o_in[2], j), l_in[2].at[j],
-                    head_col(o_out[1], j), l_out[1].at[j], rows,
-                    lambda i: take(2, j, i), lambda i: pass_on(1, j, i),
-                )
-
-            @pl.when(j == 0)
-            def _():
-                loop(0, plane, lambda p: state(DECAY, 0, p, plane, p).wait_recv())
+                hand_on(GRAM, j)
 
             head_starts(GRAM, j, gram)
             arrive(MQ, j)
@@ -705,24 +721,84 @@
                 ridge_in[pl.ds(place * per_device + j, 1), :], gram.at[j], head_col(x, j),
             )
 
+        @pl.when((last >= 0) & (plane == 1))
+        def _():
+            hand_on(CROSS, last)
+
+        @pl.when((s < 2) & (s + 1 < per_device))
+        def _():
+            forward(s + 1)
+
+        @pl.when((s == 1) & (s < per_device))
+        def _():
+            relay(1)
+
+        @pl.when((middle >= 0) & (middle < per_device) & reaches(2))
+        def _():
+            j = middle
+            bytes_of(head_col(later[2], j), QX + 1, j).wait_recv()
+            attend_far(
+                head_col(later[2], j), head_col(k, j), head_col(v, j),
+                head_col(o_out[2], j), l_out[2].at[j], rows, lambda i: pass_on(2, j, i),
+            )
+
+        @pl.when(first < per_device)
+        def _():
+            j = first
+            arrive(K, j)
+            arrive(V, j)
+            attend_own(
+                head_col(q, j), head_col(k, j), head_col(v, j), head_col(o_own, j), l_own.at[j],
+                rows,
+            )
+
+        @pl.when(s == 0)
+        def _():
+            relay(0)
+
+        @pl.when((s > 0) & (s + 2 < per_device))
+        def _():
+            forward(s + 2)
+
+        @pl.when((s > 0) & (s + 1 < per_device))
+        def _():
+            relay(s + 1)
+
+        @pl.when(s + 1 < per_device)
+        def _():
+            total_head(s + 1)
+
         @pl.when((near >= 0) & (near < per_device))
         def _():
             j = near
-            attend_own(
-                head_col(q, j), head_col(k, j), head_col(v, j), head_col(o_in[1], j),
-                l_in[1].at[j], head_col(att, j), rows,
-                lambda i: take(1, j, i), lambda i: give(ATT, j, i),
+            attend_last(
+                head_col(o_own, j), l_own.at[j], head_col(o_in[1], j), l_in[1].at[j],
+                head_col(att, j), rows, lambda i: take(1, j, i), lambda i: give(ATT, j, i),
             )
             head_totals(CROSS, j, att)
 
-        @pl.when(s == 0)
-        def _():
-            loop(0, per_device, gram_head)
-            later_planes(lambda p: state(DECAY, 0, plane, p, p).start())
+            @pl.when(jnp.logical_not(has_previous))
+            def _():
+                hand_on(CROSS, j)
+
+        @pl.when((middle >= 0) & (middle < per_device) & reaches(1))
+        def _():
+            j = middle
+            attend_middle(
+                head_col(later[1], j), head_col(k, j), head_col(v, j),
+                head_col(o_in[2], j), l_in[2].at[j],
+                head_col(o_out[1], j), l_out[1].at[j], rows,
+                lambda i: take(2, j, i), lambda i: pass_on(1, j, i),
+            )
 
         @pl.when(last >= 0)
         def _():
             j = last
+
+            @pl.when(plane > 1)
+            def _():
+                hand_on(CROSS, j)
+
             head_starts(CROSS, j, cross)
 
             def slab_out(i):
@@ -736,35 +812,38 @@
 
     loop(0, per_device + 3, step)
 
-    def finish(j):
+    def finish():
         for a in (ATT, OUT):
-            arrive(a, j)
-        for a in (Q, K, V, MK, MQ, ATT, OUT):
-            others(lambda e: remote(a, j, place, e, e).wait_send())
-
-        def block(i):
-            @pl.when(has_previous)
+            result = results[a - ATT]
+            bytes_of(result.at[:, : (g - 1) * per_device * size], a).wait_recv()
+            part = result.at[:, : per_device * size]
+            pltpu.make_async_copy(part, part, own_end.at[a - RATES]).wait()
+            bytes_of(homes[a - ATT].at[: (g - 1) * rows, :], a).wait_send()
+        for a in (Q, K, V, MK, MQ):
+            bytes_of(bufs[a].at[: (g - 1) * rows, :], a).wait_send()
+        bytes_of(rates.at[:, : g - 1], RATES).wait_send()
+
+        @pl.when(has_previous)
+        def _():
+            bytes_of(later[0], QX).wait_send()
+
+            @pl.when(reaches(1))
             def _():
-                back(1, j, i).wait_send()
-
-                @pl.when(reaches(1))
-                def _():
-                    back(2, j, i).wait_send()
-
-            for d in range(1, REACH + 1):
-
-                @pl.when(reaches(d))
-                def _(d=d):
-                    onward(PART, d, j, i).wait_send()
-                    onward(LEVEL, d, j, i).wait_send()
-
-        loop(0, g, block)
-        for a in (GRAM, CROSS):
-            later_planes(lambda p: state(a, j, plane, p, p).wait_send())
-
-    loop(0, per_device, finish)
-    later_planes(lambda p: state(DECAY, 0, plane, p, p).wait_send())
-    others(lambda e: remote(RATES, 0, place, e, e).wait_send())
+                bytes_of(later[1], QX + 1).wait_send()
+
+        for d in range(1, REACH + 1):
+
+            @pl.when(reaches(d))
+            def _(d=d):
+                bytes_of(o_out[d], PART + d - 1).wait_send()
+                bytes_of(l_out[d], LEVEL + d - 1).wait_send()
+
+        @pl.when(reaches(1))
+        def _():
+            for a in (GRAM, CROSS):
+                bytes_of(first_out[a], a).wait_send()
+
+    finish()
 
 
 def plane_body(
@@ -774,7 +853,7 @@
     heads, size = regularizer.shape
     devices = lax.axis_size("seq")
     g = WINDOW // (REACH * rows)
-    per_device, tokens, planes = heads // g, g * rows, devices // g
+    per_device, tokens = heads // g, g * rows
     per, chunks = rows // CHUNK, tokens // CHUNK
     cum = jnp.cumsum(log_decay.reshape(per, CHUNK, heads), axis=1)
     rates = jnp.concatenate([cum, input_gate.reshape(per, CHUNK, heads)], axis=0)
@@ -783,11 +862,9 @@
     vmem = pl.BlockSpec(memory_space=pltpu.VMEM)
     anywhere = pl.BlockSpec(memory_space=pl.ANY)
     tall = pltpu.VMEM((tokens, per_device * size), BF16)
-    levels = pltpu.VMEM((per_device, g, 8, rows), F32)
-    total = pltpu.VMEM((per_device, size, size), BF16)
-    totals = pltpu.VMEM((per_device, planes, size, size), BF16)
+    levels = pltpu.VMEM((per_device, g, 1, rows), F32)
+    first = pltpu.VMEM((per_device, size, size), BF16)
     states = pltpu.VMEM((per_device, chunks, size, size), BF16)
-    slots = max(g, planes)
     return pl.pallas_call(
         functools.partial(plane_kernel, devices, g),
         out_shape=(slab, slab),
@@ -797,19 +874,23 @@
         + [pltpu.VMEM((per_device, g, 4 * per, CHUNK), F32)]
         + [tall] * (2 + REACH + 2 * REACH)
         + [levels] * (2 * REACH)
-        + [total] * 2
-        + [totals] * 2
+        + [first] * 4
         + [
             pltpu.VMEM((8, size), F32),
-            pltpu.VMEM((planes, 8, size), F32),
-            pltpu.VMEM((2, per_device, chunks, size, size), F32),
+            pltpu.VMEM((2, per_device, chunks + 1, size, size), F32),
         ]
         + [states] * 2
         + [
             tall,
-            pltpu.SemaphoreType.DMA((KINDS, per_device, slots)),
-            pltpu.SemaphoreType.DMA((KINDS, per_device, slots)),
-            pltpu.SemaphoreType.DMA((KINDS, per_device)),
+            pltpu.VMEM((tokens, per_device * size), F32),
+            levels,
+            pltpu.SemaphoreType.DMA((KINDS,)),
+            pltpu.SemaphoreType.DMA((2, per_device, g)),
+            pltpu.SemaphoreType.DMA((len(BY_HEAD), per_device)),
+            pltpu.SemaphoreType.DMA((2 * REACH, per_device, g // 2)),
+            pltpu.SemaphoreType.DMA((3,)),
+            pltpu.SemaphoreType.DMA((5, per_device)),
+            pltpu.SemaphoreType.DMA((3,)),
         ],
         compiler_params=pltpu.CompilerParams(
             collective_id=0, has_side_effects=True, vmem_limit_bytes=56 * 1024 * 1024
@@ -827,6 +908,7 @@
         and mesh.shape["seq"] % g == 0
         and heads % g == 0
         and 2 <= heads // g <= 8
+        and g % 2 == 0
         and rows % CHUNK == 0
         and WAYS % (rows // CHUNK) == 0
         and g * rows % (CHUNK * WAYS) == 0

time: 120 us -> 111 us (0.925)
  Pallas kernels: 113 us -> 105 us
    pallas_call x1, Pallas kernels: 113 us -> 105 us  [plane_body(): pl.pallas_call(functools.partial(plane_kernel, devices, g), out_shape=(sl...]
where the time goes in v4:
time: 111 us
  Pallas kernels  105 us (95%)
  local copies, waits for them, and re-layouts  4.91 us (4%)
    pallas_call x1, Pallas kernels, plane_body(): pl.pallas_call(functools.partial(plane_kernel, devices, g), out_shape=(sl...  105 us
    unnamed x6, local copies, waits for them, and re-layouts  3.37 us

profile of v4, /device:TPU:29, one launch (start us, length us, event | category | flops | bytes accessed | tf_op | source)
XLA Modules:
  0.0 111.1 jit_solution(14498117182836659846)
XLA Ops:
  0.6 0.0 copy-start.1
  0.6 0.7 reshape.11
  1.4 0.0 copy-done.1
  1.4 0.1 copy.12
  1.5 0.2 reduce_window_sum.11
  1.7 0.1 copy.11
  1.8 0.6 pad.4.refs_5_
  2.4 105.3 %shard_map.95 = (bf16[256,2048]{1,0:T(8,128)(2,1)}, bf16[256,2048]{1,0:T(8,128)(2,1)}) custom-call(bf16[256,2048]{1,0:T(8,128)(2,1)} %refs_0_.1, bf16[256,2048]{1,0:T(8,128)(2,1)} %refs_1_.1, bf16[256,2048]{1,0:T(8,128)(2,1)} %refs_2_.1, bf16[256,2048]{1,0:T(8,128)(2,1)} %refs_3_.1, bf16[256,2048]{1,0:T(8,128)(2,1)} %refs_4_.1, f32[16,8,128]{2,1,0:T(8,128)} %pad.4.refs_5_, ...), custom_call_target="tpu_custom_call" | custom-call | tf_op jit(solution)/shard_map/pallas_call | solution.py:868
  107.7 0.0 copy-start
  107.7 2.4 %copy.15 = bf16[256,2048]{1,0:T(8,128)(2,1)} copy(bf16[256,2048]{1,0:T(8,128)(2,1)} %get-tuple-element.4) | data formatting | bytes 2097152
  110.1 0.0 copy-done
  110.1 1.0 copy.16
  (1 shorter events, 0.0 us)
Async XLA Ops:
  0.6 0.7 copy-start.1
  107.7 2.4 %copy-start = (bf16[256,2048]{1,0:T(8,128)(2,1)S(1)}, bf16[256,2048]{1,0:T(8,128)(2,1)}, u32[]{:S(2)}) copy-start(bf16[256,2048]{1,0:T(8,128)(2,1)} %get-tuple-element.5) | copy-start | bytes 3145732

commit v5 on v4

--- a/solution.py
+++ b/solution.py
@@ -200,7 +200,6 @@
 BF16 = jnp.bfloat16
 F32 = jnp.float32
 NT = (((1,), (1,)), ((), ()))
-TN = (((0,), (0,)), ((), ()))
 
 
 def dot(a, b, dims=None):
@@ -342,11 +341,10 @@
     return rates_ref[slab, place : place + 1, :], rates_ref[slab, per + place : per + place + 1, :]
 
 
-def tail_keys(k_ref, rates_ref, c, per):
+def tail_keys(turned_ref, rates_ref, c, per):
     cum, gate = rates_of(rates_ref, c)
-    weight = column_form(jnp.exp(cum[:, CHUNK - 1 :] - cum) * gate)
-    keys = k_ref[span(c, per), :]
-    return (keys.astype(F32) * weight).astype(BF16), jnp.exp(cum[:, CHUNK - 1 :])
+    weight = jnp.exp(cum[:, CHUNK - 1 :] - cum) * gate
+    return (turned_ref[flat(c, per)].astype(F32) * weight).astype(BF16), jnp.exp(cum[:, CHUNK - 1 :])
 
 
 def mix_of(rates_ref, c):
@@ -360,7 +358,16 @@
     return mix, jnp.exp(col)
 
 
-def state_totals(k_ref, other_ref, rates_ref, zero_ref):
+def turn_keys(k_ref, turned_ref):
+    def one(c, carry):
+        rows = pl.ds(pl.multiple_of(c * CHUNK, CHUNK), CHUNK)
+        turned_ref[c] = jnp.transpose(k_ref[rows, :])
+        return carry
+
+    lax.fori_loop(0, turned_ref.shape[0], one, 0, unroll=4)
+
+
+def state_totals(turned_ref, other_ref, rates_ref, zero_ref):
     per = rates_ref.shape[1] // 4
     chunks = rates_ref.shape[0] * per
 
@@ -368,8 +375,8 @@
         state, decay = carry
         for c in chunk_ids(g, per):
             zero_ref[flat(c, per)] = state
-            keys, end = tail_keys(k_ref, rates_ref, c, per)
-            state = end * state + dot(keys, other_ref[span(c, per), :], TN)
+            keys, end = tail_keys(turned_ref, rates_ref, c, per)
+            state = end * state + dot(keys, other_ref[span(c, per), :])
             decay = decay * end
         return state, decay
 
@@ -394,7 +401,7 @@
     lax.fori_loop(0, chunks // WAYS, step, first_ref[...].astype(F32))
 
 
-def solve_all(q_ref, k_ref, rates_ref, ridge_ref, gram_ref, x_ref):
+def solve_all(q_ref, k_ref, turned_ref, rates_ref, ridge_ref, gram_ref, x_ref):
     per = rates_ref.shape[1] // 4
     chunks = rates_ref.shape[0] * per
     ways = math.gcd(chunks, 8)
@@ -413,7 +420,7 @@
             starts.append(jnp.exp(cum))
             keys.append(k_ref[span(c, per), :])
             sides.append(
-                jnp.concatenate([gram_ref[flat(c, per)], jnp.transpose(keys[-1])], axis=1)
+                jnp.concatenate([gram_ref[flat(c, per)], turned_ref[flat(c, per)]], axis=1)
             )
             q = jnp.transpose(q_ref[span(c, per), :]).astype(F32)
             state.append((jnp.zeros_like(q), q, q, jnp.sum(q * q, axis=0, keepdims=True)))
@@ -482,9 +489,9 @@
     l_out, l_in = (None,) + refs[23:25], (None,) + refs[25:27]
     first_out, first_in = {GRAM: refs[27], CROSS: refs[28]}, {GRAM: refs[29], CROSS: refs[30]}
     decays, zero = refs[31:33]
-    gram, cross, x = refs[33:36]
-    o_own, l_own = refs[36:38]
-    send, by_block, by_head, by_pair, at_end, own, own_end = refs[38:45]
+    gram, cross, turned, x = refs[33:37]
+    o_own, l_own = refs[37:39]
+    send, by_block, by_head, by_pair, at_end, own, own_end = refs[39:46]
     q, k, v, mk, mq = bufs
     att, out = homes
     rows, size = ins[0].shape[0], ridge_in.shape[1]
@@ -671,7 +678,7 @@
 
     def head_totals(a, j, others_ref):
         return state_totals(
-            head_col(mk, j), head_col(others_ref, j), rates.at[j], zero.at[a - GRAM, j]
+            turned.at[j], head_col(others_ref, j), rates.at[j], zero.at[a - GRAM, j]
         )
 
     def hand_on(a, j):
@@ -691,12 +698,31 @@
 
     def total_head(j):
         arrive(MK, j)
+        turn_keys(head_col(mk, j), turned.at[j])
         decay = head_totals(GRAM, j, mk)
         decays[pl.ds(j, 1), :] = jnp.broadcast_to(decay, (1, size))
 
         @pl.when(jnp.logical_not(has_previous))
         def _():
             hand_on(GRAM, j)
+
+    def far_head(j):
+        bytes_of(head_col(later[2], j), QX + 1, j).wait_recv()
+        attend_far(
+            head_col(later[2], j), head_col(k, j), head_col(v, j),
+            head_col(o_out[2], j), l_out[2].at[j], rows, lambda i: pass_on(2, j, i),
+        )
+
+    def merge_head(j):
+        attend_last(
+            head_col(o_own, j), l_own.at[j], head_col(o_in[1], j), l_in[1].at[j],
+            head_col(att, j), rows, lambda i: take(1, j, i), lambda i: give(ATT, j, i),
+        )
+        head_totals(CROSS, j, att)
+
+        @pl.when(jnp.logical_not(has_previous))
+        def _():
+            hand_on(CROSS, j)
 
     def step(s):
         first, middle, near, last = s, s - 1, s - 2, s - 3
@@ -717,7 +743,7 @@
             head_starts(GRAM, j, gram)
             arrive(MQ, j)
             solve_all(
-                head_col(mq, j), head_col(mk, j), rates.at[j],
+                head_col(mq, j), head_col(mk, j), turned.at[j], rates.at[j],
                 ridge_in[pl.ds(place * per_device + j, 1), :], gram.at[j], head_col(x, j),
             )
 
@@ -733,14 +759,9 @@
         def _():
             relay(1)
 
-        @pl.when((middle >= 0) & (middle < per_device) & reaches(2))
-        def _():
-            j = middle
-            bytes_of(head_col(later[2], j), QX + 1, j).wait_recv()
-            attend_far(
-                head_col(later[2], j), head_col(k, j), head_col(v, j),
-                head_col(o_out[2], j), l_out[2].at[j], rows, lambda i: pass_on(2, j, i),
-            )
+        @pl.when((middle >= 0) & (middle < per_device - 1) & reaches(2))
+        def _():
+            far_head(middle)
 
         @pl.when(first < per_device)
         def _():
@@ -768,18 +789,13 @@
         def _():
             total_head(s + 1)
 
-        @pl.when((near >= 0) & (near < per_device))
-        def _():
-            j = near
-            attend_last(
-                head_col(o_own, j), l_own.at[j], head_col(o_in[1], j), l_in[1].at[j],
-                head_col(att, j), rows, lambda i: take(1, j, i), lambda i: give(ATT, j, i),
-            )
-            head_totals(CROSS, j, att)
-
-            @pl.when(jnp.logical_not(has_previous))
-            def _():
-                hand_on(CROSS, j)
+        @pl.when((first == per_device - 1) & reaches(2))
+        def _():
+            far_head(first)
+
+        @pl.when((near >= 0) & (near < per_device) & (plane == 0))
+        def _():
+            merge_head(near)
 
         @pl.when((middle >= 0) & (middle < per_device) & reaches(1))
         def _():
@@ -790,6 +806,10 @@
                 head_col(o_out[1], j), l_out[1].at[j], rows,
                 lambda i: take(2, j, i), lambda i: pass_on(1, j, i),
             )
+
+        @pl.when((near >= 0) & (near < per_device) & has_previous)
+        def _():
+            merge_head(near)
 
         @pl.when(last >= 0)
         def _():
@@ -879,7 +899,7 @@
             pltpu.VMEM((8, size), F32),
             pltpu.VMEM((2, per_device, chunks + 1, size, size), F32),
         ]
-        + [states] * 2
+        + [states] * 3
         + [
             tall,
             pltpu.VMEM((tokens, per_device * size), F32),

time: 111 us -> 109 us (0.982)
  Pallas kernels: 105 us -> 103 us
    pallas_call x1, Pallas kernels: 105 us -> 103 us  [plane_body(): pl.pallas_call(functools.partial(plane_kernel, devices, g), out_shape=(sl...]
where the time goes in v5:
time: 109 us
  Pallas kernels  103 us (94%)
  local copies, waits for them, and re-layouts  4.91 us (5%)
    pallas_call x1, Pallas kernels, plane_body(): pl.pallas_call(functools.partial(plane_kernel, devices, g), out_shape=(sl...  103 us
    unnamed x6, local copies, waits for them, and re-layouts  3.37 us

profile of v5, /device:TPU:29, one launch (start us, length us, event | category | flops | bytes accessed | tf_op | source)
XLA Modules:
  0.0 109.1 jit_solution(2726547429904735694)
XLA Ops:
  0.6 0.0 copy-start.1
  0.6 0.7 reshape.11
  1.4 0.0 copy-done.1
  1.4 0.1 copy.12
  1.5 0.2 reduce_window_sum.11
  1.7 0.1 copy.11
  1.8 0.6 pad.4.refs_5_
  2.4 103.3 %shard_map.95 = (bf16[256,2048]{1,0:T(8,128)(2,1)}, bf16[256,2048]{1,0:T(8,128)(2,1)}) custom-call(bf16[256,2048]{1,0:T(8,128)(2,1)} %refs_0_.1, bf16[256,2048]{1,0:T(8,128)(2,1)} %refs_1_.1, bf16[256,2048]{1,0:T(8,128)(2,1)} %refs_2_.1, bf16[256,2048]{1,0:T(8,128)(2,1)} %refs_3_.1, bf16[256,2048]{1,0:T(8,128)(2,1)} %refs_4_.1, f32[16,8,128]{2,1,0:T(8,128)} %pad.4.refs_5_, ...), custom_call_target="tpu_custom_call" | custom-call | tf_op jit(solution)/shard_map/pallas_call | solution.py:888
  105.8 0.0 copy-start
  105.8 2.4 %copy.15 = bf16[256,2048]{1,0:T(8,128)(2,1)} copy(bf16[256,2048]{1,0:T(8,128)(2,1)} %get-tuple-element.4) | data formatting | bytes 2097152
  108.2 0.0 copy-done
  108.2 1.0 copy.16
  (1 shorter events, 0.0 us)
Async XLA Ops:
  0.6 0.7 copy-start.1
  105.8 2.4 %copy-start = (bf16[256,2048]{1,0:T(8,128)(2,1)S(1)}, bf16[256,2048]{1,0:T(8,128)(2,1)}, u32[]{:S(2)}) copy-start(bf16[256,2048]{1,0:T(8,128)(2,1)} %get-tuple-element.5) | copy-start | bytes 3145732

commit v6 on v5

--- a/solution.py
+++ b/solution.py
@@ -471,7 +471,7 @@
 
 
 def push_order(heads):
-    order = [(MK, 0), (Q, 0), (MQ, 0), (Q, 1), (K, 0), (V, 0)]
+    order = [(Q, 0), (MK, 0), (MQ, 0), (K, 0), (V, 0), (Q, 1)]
     for j in range(1, heads):
         order += [(MK, j), (MQ, j)]
         order += [(Q, 2)] if j == 1 and heads > 2 else []
@@ -876,8 +876,8 @@
     per_device, tokens = heads // g, g * rows
     per, chunks = rows // CHUNK, tokens // CHUNK
     cum = jnp.cumsum(log_decay.reshape(per, CHUNK, heads), axis=1)
-    rates = jnp.concatenate([cum, input_gate.reshape(per, CHUNK, heads)], axis=0)
-    rates = jnp.pad(jnp.transpose(rates, (2, 0, 1)), ((0, 0), (0, 2 * per), (0, 0)))
+    rates = jnp.concatenate([cum, input_gate.reshape(per, CHUNK, heads)] * 2, axis=0)
+    rates = jnp.transpose(rates, (2, 0, 1))
     slab = jax.ShapeDtypeStruct((rows, heads * size), BF16)
     vmem = pl.BlockSpec(memory_space=pltpu.VMEM)
     anywhere = pl.BlockSpec(memory_space=pl.ANY)

time: 109 us -> 109 us (level)
  no operation moved by 1% of the time
where the time goes in v6:
time: 109 us
  Pallas kernels  103 us (94%)
  local copies, waits for them, and re-layouts  4.27 us (4%)
    pallas_call x1, Pallas kernels, plane_body(): pl.pallas_call(functools.partial(plane_kernel, devices, g), out_shape=(sl...  103 us
    unnamed x6, local copies, waits for them, and re-layouts  3.37 us

profile of v6, /device:TPU:29, one launch (start us, length us, event | category | flops | bytes accessed | tf_op | source)
XLA Modules:
  0.0 109.1 jit_solution(16666327633503112493)
XLA Ops:
  0.6 0.0 copy-start.1
  0.6 0.7 reshape.11
  1.4 0.0 copy-done.1
  1.4 0.1 copy.13
  1.5 0.2 reduce_window_sum.11
  1.7 0.1 copy.11
  1.7 0.7 maximum_bitcast_fusion.refs_5_
  2.4 103.3 %shard_map.95 = (bf16[256,2048]{1,0:T(8,128)(2,1)}, bf16[256,2048]{1,0:T(8,128)(2,1)}) custom-call(bf16[256,2048]{1,0:T(8,128)(2,1)} %refs_0_.1, bf16[256,2048]{1,0:T(8,128)(2,1)} %refs_1_.1, bf16[256,2048]{1,0:T(8,128)(2,1)} %refs_2_.1, bf16[256,2048]{1,0:T(8,128)(2,1)} %refs_3_.1, bf16[256,2048]{1,0:T(8,128)(2,1)} %refs_4_.1, ...), custom_call_target="tpu_custom_call" | custom-call | tf_op jit(solution)/shard_map/pallas_call | solution.py:888
  105.8 0.0 copy-start
  105.8 2.4 %copy.16 = bf16[256,2048]{1,0:T(8,128)(2,1)} copy(bf16[256,2048]{1,0:T(8,128)(2,1)} %get-tuple-element.4) | data formatting | bytes 2097152
  108.2 0.0 copy-done
  108.2 1.0 copy.17
Async XLA Ops:
  0.6 0.7 copy-start.1
  105.8 2.4 %copy-start = (bf16[256,2048]{1,0:T(8,128)(2,1)S(1)}, bf16[256,2048]{1,0:T(8,128)(2,1)}, u32[]{:S(2)}) copy-start(bf16[256,2048]{1,0:T(8,128)(2,1)} %get-tuple-element.5) | copy-start | bytes 3145732
